TPU v7x, 8 devices: a whole 2x2x1 slice. The times are simulated.
8 devices in a mesh: dp: 1 (over z), row: 2 (over y), col: 2 (over x), core: 2 (over core).
Axes of the slice: x: 2, y: 2, z: 1, core: 2. Of those that a mesh axis runs over, the one named last changes fastest.
Arguments:
- x: bfloat16 [1024, 896], P(('dp', 'row', 'col', 'core'))
- route_idx: int32 [1024, 8], P(('dp', 'row', 'col', 'core'))
- gates: float32 [1024, 8], P(('dp', 'row', 'col', 'core'))
- w1: bfloat16 [256, 896, 256], P(('row', 'col', 'core'))
- w3: bfloat16 [256, 896, 256], P(('row', 'col', 'core'))
- w2: bfloat16 [256, 256, 896], P(('row', 'col', 'core'))
- dy: bfloat16 [1024, 896], P(('dp', 'row', 'col', 'core'))
Outputs:
- output 1: bfloat16 [1024, 896], P(('dp', 'row', 'col', 'core'))
- output 2: bfloat16 [1024, 896], P(('dp', 'row', 'col', 'core'))
- output 3: float32 [1024, 8], P(('dp', 'row', 'col', 'core'))
- output 4: float32 [256, 896, 256], P(('dp', 'row', 'col', 'core'))
- output 5: float32 [256, 896, 256], P(('dp', 'row', 'col', 'core'))
- output 6: float32 [256, 256, 896], P(('dp', 'row', 'col', 'core'))
All inputs are finite; a program needn't handle non-finite values.
Results may differ from a plain program's by a relative error of at most 0.0104406.
Values are sent between devices in bfloat16 or wider.
A program may use at most 1 GiB of HBM per device.

v0:
```python
import functools

import jax
import jax.numpy as jnp
from jax import lax
from jax.experimental import pallas as pl
from jax.experimental.pallas import tpu as pltpu
from jax.sharding import PartitionSpec as P

MESH = pl.DeviceIdType.MESH
F32 = jnp.float32
BF = jnp.bfloat16
ROWS = 16
SLOTS = 5
DIM0 = (((0,), (0,)), ((), ()))
DIM1 = (((1,), (1,)), ((), ()))
ANY = pl.BlockSpec(memory_space=pl.ANY)


def _dot(a, b, dims=(((1,), (0,)), ((), ()))):
    return lax.dot_general(a, b, dims, preferred_element_type=F32)


def _core_kernel(x_hbm, dy_hbm, tab_hbm, w1_hbm, w3_hbm, w2_hbm,
                 xg_out, q_out, act_out, du_out, dv_out, y_out, dg_out, dx0, dx1, dx2, dx3,
                 x_all, dy_all, tab_all, xg, q, o, u, v, act, onehot, gate3,
                 w1, w3, w2, y_send, y_own, y_chip, y_far, d_send, d_own, d_chip, dg_send, dg_all, y_v, dg_v,
                 in_sem, w_sem, out_sem,
                 xs_sem, xr_sem, ys_sem, yr_sem, ts_sem, tr_sem,
                 yc_s, yc_r, yf_s, yf_r, dc_s, dc_r, gs_sem, gr_sem):
    row, col, core = lax.axis_index('row'), lax.axis_index('col'), lax.axis_index('core')
    el, dm, fh = w1_hbm.shape
    td = x_hbm.shape[0]
    top = tab_hbm.shape[0] // 2
    n_src = x_all.shape[0]

    def peer(k):
        r = 1 - row if k & 4 else row
        c = 1 - col if k & 2 else col
        h = 1 - core if k & 1 else core
        return {'row': r, 'col': c, 'core': h}, r * 4 + c * 2 + h

    me = peer(0)[1]

    own = [pltpu.make_async_copy(a, b.at[me], in_sem.at[i])
           for i, (a, b) in enumerate(((tab_hbm, tab_all), (x_hbm, x_all), (dy_hbm, dy_all)))]
    for c in own:
        c.start()

    def weights(i):
        e, slot = i % el, i % SLOTS
        return [pltpu.make_async_copy(a.at[e], b.at[slot], w_sem.at[j, slot])
                for j, (a, b) in enumerate(((w1_hbm, w1), (w3_hbm, w3), (w2_hbm, w2)))]

    for i in range(SLOTS):
        for c in weights(i):
            c.start()

    barrier = pltpu.get_barrier_semaphore()
    for k in range(1, n_src):
        pl.semaphore_signal(barrier, inc=1, device_id=peer(k)[0], device_id_type=MESH)
    pl.semaphore_wait(barrier, n_src - 1)

    def send(src, dst, s_sem, r_sem, k):
        c = pltpu.make_async_remote_copy(src_ref=src, dst_ref=dst, send_sem=s_sem, recv_sem=r_sem,
                                         device_id=peer(k)[0], device_id_type=MESH)
        c.start()
        return c

    def arrive(dst, s_sem, r_sem):
        pltpu.make_async_remote_copy(src_ref=dst, dst_ref=dst, send_sem=s_sem, recv_sem=r_sem,
                                     device_id=peer(1)[0], device_id_type=MESH).wait_recv()

    sent = []
    own[0].wait()
    for k in range(1, n_src):
        sent.append(send(tab_all.at[me], tab_all.at[me], ts_sem.at[k], tr_sem.at[me], k))
    own[1].wait()
    for k in (2, 4, 6, 1):
        sent.append(send(x_all.at[me], x_all.at[me], xs_sem.at[k], xr_sem.at[me], k))
    own[2].wait()
    for k in (2, 4, 6, 1):
        sent.append(send(dy_all.at[me], dy_all.at[me], ys_sem.at[k], yr_sem.at[me], k))

    for k in range(1, n_src):
        s = peer(k)[1]
        arrive(tab_all.at[s], ts_sem.at[k], tr_sem.at[s])

    experts = (lax.broadcasted_iota(jnp.int32, (el, td), 0) + me * el).astype(F32)
    before = (lax.broadcasted_iota(jnp.int32, (td, td), 0) < lax.broadcasted_iota(jnp.int32, (td, td), 1))
    before = jnp.where(before, 1.0, 0.0).astype(BF)
    place = lax.broadcasted_iota(jnp.int32, (el, ROWS, td), 1).astype(F32)

    def tables(s, _):
        hit = jnp.zeros((el, td), F32)
        gate = jnp.zeros((el, td), F32)
        for j in range(top):
            m = tab_all[s, j:j + 1, :] == experts
            hit = jnp.where(m, 1.0, hit)
            gate = jnp.where(m, tab_all[s, top + j:top + j + 1, :], gate)
        rank = _dot(hit.astype(BF), before)
        rank = jnp.where(hit > 0, rank, -1.0)
        sel = jnp.broadcast_to(rank[:, None, :], place.shape) == place
        onehot[s] = jnp.where(sel, 1.0, 0.0).astype(BF).reshape(el * ROWS, td)
        g = jnp.where(sel, jnp.broadcast_to(gate[:, None, :], place.shape), 0.0).reshape(el * ROWS, td)
        for i in range(3):
            part = g.astype(BF)
            gate3[s, :, i * td:(i + 1) * td] = part
            g = g - part.astype(F32)
        return 0

    lax.fori_loop(0, n_src, tables, 0)

    def rows_of(s):
        return pl.ds(pl.multiple_of(s * ROWS, ROWS), ROWS)

    for k in (0, 1, 2, 4, 6, 3, 5, 7):
        s = peer(k)[1]
        if k:
            arrive(x_all.at[s], xs_sem.at[k], xr_sem.at[s])
        if k in (2, 4, 6):
            sent.append(send(x_all.at[s], x_all.at[s], xs_sem.at[k + 1], xr_sem.at[s], 1))
        xg[:, rows_of(s), :] = _dot(onehot[s], x_all[s]).astype(BF).reshape(el, ROWS, dm)
    outs = [pltpu.make_async_copy(xg, xg_out, out_sem.at[0])]
    outs[0].start()

    def forward(e, _):
        slot = e % SLOTS
        for c in weights(e):
            c.wait()
        xe = xg[e]
        ue = _dot(xe, w1[slot]).astype(BF)
        ve = _dot(xe, w3[slot]).astype(BF)
        u[e] = ue
        v[e] = ve
        uf = ue.astype(F32)
        a = (uf * jax.nn.sigmoid(uf) * ve.astype(F32)).astype(BF)
        act[e] = a
        o[e] = _dot(a, w2[slot]).astype(BF)
        for c in weights(e + SLOTS):
            c.start()
        return 0

    half = el // 2
    lax.fori_loop(0, half, forward, 0)
    for k in (2, 4, 6):
        s = peer(k)[1]
        arrive(dy_all.at[s], ys_sem.at[k], yr_sem.at[s])
        sent.append(send(dy_all.at[s], dy_all.at[s], ys_sem.at[k + 1], yr_sem.at[s], 1))
    lax.fori_loop(half, el, forward, 0)
    outs.append(pltpu.make_async_copy(act, act_out, out_sem.at[1]))
    outs[1].start()

    def y_part(s):
        z = _dot(gate3[s], o[:, rows_of(s), :].reshape(el * ROWS, dm), DIM0)
        return z[:td] + z[td:2 * td] + z[2 * td:]

    for j in range(4):
        y_send[j] = y_part(peer(2 * j + 1)[1])
        sent.append(send(y_send.at[j], y_chip.at[j], yc_s.at[j], yc_r.at[j], 1))
    for j in range(4):
        y_own[j] = y_part(peer(2 * j)[1])
    for j in (3, 1, 2, 0):
        arrive(y_chip.at[j], yc_s.at[j], yc_r.at[j])
        y_own[j] = y_own[j] + y_chip[j]
        if j:
            sent.append(send(y_own.at[j], y_far.at[j - 1], yf_s.at[j - 1], yf_r.at[j - 1], 2 * j))

    def dispatch_dy(s, k):
        d = _dot(onehot[s], dy_all[s])
        os = o[:, rows_of(s), :].reshape(el * ROWS, dm).astype(F32)
        hot = onehot[s].astype(F32)
        dg = jnp.sum(d * os, axis=1, keepdims=True)
        dgt = jnp.sum((hot * dg).reshape(el, ROWS, td), axis=1)
        g = gate3[s]
        g = g[:, :td].astype(F32) + g[:, td:2 * td].astype(F32) + g[:, 2 * td:].astype(F32)
        g = jnp.sum(g, axis=1, keepdims=True)
        q[:, rows_of(s), :] = (g * d).astype(BF).reshape(el, ROWS, dm)
        for j in range(top):
            m = tab_all[s, j:j + 1, :] == experts
            dg_send[s, j:j + 1, :] = jnp.sum(jnp.where(m, dgt, 0.0), axis=0, keepdims=True)

    for k in (0, 1, 2, 4, 6, 3, 5, 7):
        s = peer(k)[1]
        if k in (1, 3, 5, 7):
            arrive(dy_all.at[s], ys_sem.at[k], yr_sem.at[s])
        dispatch_dy(s, k)
        if k:
            sent.append(send(dg_send.at[s], dg_all.at[me], gs_sem.at[k], gr_sem.at[me], k))
        else:
            dg_all[me] = dg_send[s]
    outs.append(pltpu.make_async_copy(q, q_out, out_sem.at[2]))
    outs[2].start()

    def backward(i, _):
        e = i - el
        slot = i % SLOTS
        for c in weights(i):
            c.wait()
        da = _dot(q[e], w2[slot], DIM1).astype(BF).astype(F32)
        uf = u[e].astype(F32)
        vf = v[e].astype(F32)
        sg = jax.nn.sigmoid(uf)
        du = (da * vf * sg * (1 + uf * (1 - sg))).astype(BF)
        dv = (da * (uf * sg)).astype(BF)
        u[e] = du
        v[e] = dv
        o[e] = (_dot(du, w1[slot], DIM1) + _dot(dv, w3[slot], DIM1)).astype(BF)

        @pl.when(i + SLOTS < 2 * el)
        def _():
            for c in weights(i + SLOTS):
                c.start()
        return 0

    lax.fori_loop(el, 2 * el, backward, 0)
    for i, (a, b) in enumerate(((u, du_out), (v, dv_out))):
        outs.append(pltpu.make_async_copy(a, b, out_sem.at[3 + i]))
        outs[-1].start()

    def dx_part(s):
        return _dot(onehot[s], o[:, rows_of(s), :].reshape(el * ROWS, dm), DIM0)

    for j in range(4):
        d_send[j] = dx_part(peer(2 * j + 1)[1])
        sent.append(send(d_send.at[j], d_chip.at[j], dc_s.at[j], dc_r.at[j], 1))
    for j in range(4):
        d_own[j] = dx_part(peer(2 * j)[1])

    for j in range(3):
        arrive(y_far.at[j], yf_s.at[j], yf_r.at[j])
    y_v[...] = (y_own[0] + y_far[0] + y_far[1] + y_far[2]).astype(BF)
    for k in range(1, n_src):
        s = peer(k)[1]
        arrive(dg_all.at[s], gs_sem.at[k], gr_sem.at[s])
    dg_v[...] = jnp.sum(dg_all[...], axis=0)
    outs.append(pltpu.make_async_copy(y_v, y_out, out_sem.at[5]))
    outs[-1].start()
    outs.append(pltpu.make_async_copy(dg_v, dg_out, out_sem.at[6]))
    outs[-1].start()

    for j, out in ((3, dx3), (1, dx1), (2, dx2), (0, dx0)):
        arrive(d_chip.at[j], dc_s.at[j], dc_r.at[j])
        d_own[j] = d_own[j] + d_chip[j]
        outs.append(pltpu.make_async_copy(d_own.at[j], out, out_sem.at[7 + j]))
        outs[-1].start()

    for c in sent:
        c.wait_send()
    for c in outs:
        c.wait()


def _grad_kernel(xg, q, act, du, dv, dw1, dw3, dw2):
    for i in range(xg.shape[0]):
        dw1[i] = _dot(xg[i], du[i], DIM0)
        dw3[i] = _dot(xg[i], dv[i], DIM0)
        dw2[i] = _dot(act[i], q[i], DIM0)


def solution(mesh):
    ep = ('row', 'col', 'core')
    n_src = mesh.shape['row'] * mesh.shape['col'] * mesh.shape['core']
    tspec = P(('dp',) + ep, None)
    wspec = P(ep, None, None)
    gspec = P(('dp',) + ep, None, None)

    def body(x, route_idx, gates, w1, w3, w2, dy):
        td, top = route_idx.shape
        el, dm, fh = w1.shape
        er = n_src * ROWS
        tab = jnp.concatenate([route_idx.T.astype(F32), gates.T], axis=0)
        sds = jax.ShapeDtypeStruct
        dma = pltpu.SemaphoreType.DMA
        block = (td, dm)
        flops = 2 * el * er * dm * fh * 6
        xg, q, act, du, dv, y, dg, dx0, dx1, dx2, dx3 = pl.pallas_call(
            _core_kernel,
            name='moe_core',
            out_shape=[sds((el, er, dm), BF), sds((el, er, dm), BF)] + [sds((el, er, fh), BF)] * 3
            + [sds(block, BF), sds((top, td), F32)] + [sds(block, F32)] * 4,
            in_specs=[ANY] * 6,
            out_specs=[ANY] * 11,
            scratch_shapes=[
                pltpu.VMEM((n_src,) + block, BF), pltpu.VMEM((n_src,) + block, BF), pltpu.VMEM((n_src, 2 * top, td), F32),
                pltpu.VMEM((el, er, dm), BF), pltpu.VMEM((el, er, dm), BF), pltpu.VMEM((el, er, dm), BF),
                pltpu.VMEM((el, er, fh), BF), pltpu.VMEM((el, er, fh), BF), pltpu.VMEM((el, er, fh), BF),
                pltpu.VMEM((n_src, el * ROWS, td), BF), pltpu.VMEM((n_src, el * ROWS, 3 * td), BF),
                pltpu.VMEM((SLOTS, dm, fh), BF), pltpu.VMEM((SLOTS, dm, fh), BF), pltpu.VMEM((SLOTS, fh, dm), BF),
                pltpu.VMEM((4,) + block, F32), pltpu.VMEM((4,) + block, F32), pltpu.VMEM((4,) + block, F32),
                pltpu.VMEM((3,) + block, F32),
                pltpu.VMEM((4,) + block, F32), pltpu.VMEM((4,) + block, F32), pltpu.VMEM((4,) + block, F32),
                pltpu.VMEM((n_src, top, td), F32), pltpu.VMEM((n_src, top, td), F32),
                pltpu.VMEM(block, BF), pltpu.VMEM((top, td), F32),
                dma((3,)), dma((3, SLOTS)), dma((11,)),
                dma((8,)), dma((8,)), dma((8,)), dma((8,)), dma((8,)), dma((8,)),
                dma((4,)), dma((4,)), dma((3,)), dma((3,)), dma((4,)), dma((4,)), dma((8,)), dma((8,)),
            ],
            compiler_params=pltpu.CompilerParams(collective_id=0, has_side_effects=True, vmem_limit_bytes=67043328),
            cost_estimate=pl.CostEstimate(flops=flops, bytes_accessed=88 << 20, transcendentals=0),
        )(x, dy, tab, w1, w3, w2)

        def swap(a, k):
            return lax.ppermute(a, ep, [(i, i ^ k) for i in range(n_src)])

        far = [swap(dx3, 6), swap(dx1, 2), swap(dx2, 4)]
        per = 2
        spec = lambda a, b: pl.BlockSpec((per, a, b), lambda i: (i, 0, 0))
        dw1, dw3, dw2 = pl.pallas_call(
            _grad_kernel,
            name='moe_grad',
            grid=(el // per,),
            out_shape=[sds((el, dm, fh), F32), sds((el, dm, fh), F32), sds((el, fh, dm), F32)],
            in_specs=[spec(er, dm), spec(er, dm), spec(er, fh), spec(er, fh), spec(er, fh)],
            out_specs=[spec(dm, fh), spec(dm, fh), spec(fh, dm)],
            compiler_params=pltpu.CompilerParams(vmem_limit_bytes=62 << 20),
            cost_estimate=pl.CostEstimate(flops=2 * el * er * dm * fh * 3, bytes_accessed=110 << 20, transcendentals=0),
        )(xg, q, act, du, dv)
        dx = (dx0 + far[0] + far[1] + far[2]).astype(BF)
        return y, dx, dg.T, dw1, dw3, dw2

    return jax.shard_map(body, mesh=mesh, in_specs=(tspec, tspec, tspec, wspec, wspec, wspec, tspec),
                         out_specs=(tspec, tspec, tspec, gspec, gspec, gspec), check_vma=False)
```

profile of v0, /device:TPU:0, one launch (start us, length us, event | category | flops | bytes accessed | tf_op | source)
XLA Modules:
  0.0 123.9 jit_solution(935338498080638613)
XLA Ops:
  0.6 0.7 convert_bitcast_fusion
  1.3 1.3 %pad_maximum_fusion.tab_hbm = f32[16,128]{1,0:T(8,128)} fusion(f32[8,128]{1,0:T(8,128)} %bitcast.5, f32[8,128]{1,0:T(8,128)S(1)} %convert_bitcast_fusion), kind=kLoop, calls=%fused_computation.1 | loop fusion | flops 2048 | bytes 16384 | tf_op jit(solution)/shard_map/concatenate | solution.py:272
  2.6 79.3 %moe_core.1 = (bf16[32,128,896]{2,1,0:T(8,128)(2,1)}, bf16[32,128,896]{2,1,0:T(8,128)(2,1)}, bf16[32,128,256]{2,1,0:T(8,128)(2,1)}, bf16[32,128,256]{2,1,0:T(8,1...) custom-call(bf16[128,896]{1,0:T(8,128)(2,1)} %x_hbm.1, ...), custom_call_target="tpu_custom_call" | custom-call | flops 11274289152 | bytes 92274688 | tf_op jit(solution)/shard_map/moe_core/pallas_call | solution.py:277
  81.9 0.0 copy-start
  81.9 0.0 copy-start.1
  81.9 0.6 collective-permute-start
  82.5 1.4 %collective-permute-start.1 = (f32[128,896]{1,0:T(8,128)}, f32[128,896]{1,0:T(8,128)S(1)}, u32[]{:S(2)}, u32[]{:S(2)}) collective-permute-start(f32[128,896]{1,0:T(8,128)} %get-tuple-element.23), channel_id=1, source_target_pairs={{0,2},{1,3},{2,0},{3,1},{4,6},{5,7},{6,4},{7,5}} | collective-permute-start | bytes 1376264 | tf_op jit(solution)/shard_map/ppermute | solution.py:304
  83.9 1.5 %collective-permute-start.2 = (f32[128,896]{1,0:T(8,128)}, f32[128,896]{1,0:T(8,128)S(1)}, u32[]{:S(2)}, u32[]{:S(2)}) collective-permute-start(f32[128,896]{1,0:T(8,128)} %get-tuple-element.24), channel_id=1, source_target_pairs={{0,4},{1,5},{2,6},{3,7},{4,0},{5,1},{6,2},{7,3}} | collective-permute-start | bytes 1376264 | tf_op jit(solution)/shard_map/ppermute | solution.py:304
  85.4 35.5 %moe_grad.1 = (f32[32,896,256]{2,1,0:T(8,128)}, f32[32,896,256]{2,1,0:T(8,128)}, f32[32,256,896]{2,1,0:T(8,128)}) custom-call(bf16[32,128,896]{2,1,0:T(8,128)(2,1)} %get-tuple-element.26.xg, bf16[32,128,896]{2,1,0:T(8,128)(2,1)} %get-tuple-element.27.q, bf16[32,128,256]{2,1,0:T(8,128)(2,1)} %get-tuple-element.28.act, ...), custom_call_target="tpu_custom_call" | custom-call | flops 5637144576 | bytes 115343360 | tf_op jit(solution)/shard_map/moe_grad/pallas_call | solution.py:309
  120.9 0.0 collective-permute-done
  120.9 0.0 collective-permute-done.1
  120.9 0.0 collective-permute-done.2
  120.9 0.0 copy-done
  120.9 0.8 add_convert_fusion
  121.7 1.6 %copy.15 = bf16[128,896]{1,0:T(8,128)(2,1)} copy(bf16[128,896]{1,0:T(8,128)(2,1)} %get-tuple-element.40) | data formatting | bytes 458752
  123.3 0.0 copy-done.1
  123.3 0.6 copy.16
Async XLA Ops:
  81.9 39.0 %copy-start = (f32[128,896]{1,0:T(8,128)S(1)}, f32[128,896]{1,0:T(8,128)}, u32[]{:S(2)}) copy-start(f32[128,896]{1,0:T(8,128)} %get-tuple-element.21) | copy-start | bytes 1376260
  81.9 41.4 %copy-start.1 = (f32[8,128]{1,0:T(8,128)S(1)}, f32[8,128]{1,0:T(8,128)}, u32[]{:S(2)}) copy-start(f32[8,128]{1,0:T(8,128)} %get-tuple-element.25) | copy-start | bytes 12292
  81.9 39.0 %collective-permute-start = (f32[128,896]{1,0:T(8,128)}, f32[128,896]{1,0:T(8,128)S(1)}, u32[]{:S(2)}, u32[]{:S(2)}) collective-permute-start(f32[128,896]{1,0:T(8,128)} %get-tuple-element.22), channel_id=1, source_target_pairs={{0,6},{1,7},{2,4},{3,5},{4,2},{5,3},{6,0},{7,1}} | collective-permute-start | bytes 1376264 | tf_op jit(solution)/shard_map/ppermute | solution.py:304
  82.5 38.4 %collective-permute-start.1 = (f32[128,896]{1,0:T(8,128)}, f32[128,896]{1,0:T(8,128)S(1)}, u32[]{:S(2)}, u32[]{:S(2)}) collective-permute-start(f32[128,896]{1,0:T(8,128)} %get-tuple-element.23), channel_id=1, source_target_pairs={{0,2},{1,3},{2,0},{3,1},{4,6},{5,7},{6,4},{7,5}} | collective-permute-start | bytes 1376264 | tf_op jit(solution)/shard_map/ppermute | solution.py:304
  83.9 37.0 %collective-permute-start.2 = (f32[128,896]{1,0:T(8,128)}, f32[128,896]{1,0:T(8,128)S(1)}, u32[]{:S(2)}, u32[]{:S(2)}) collective-permute-start(f32[128,896]{1,0:T(8,128)} %get-tuple-element.24), channel_id=1, source_target_pairs={{0,4},{1,5},{2,6},{3,7},{4,0},{5,1},{6,2},{7,3}} | collective-permute-start | bytes 1376264 | tf_op jit(solution)/shard_map/ppermute | solution.py:304
where the time goes:
time: 125 us; the launch traced here: 124 us
  Pallas kernels  115 us (92%)
  starting transfers between devices  3.51 us (3%)
  other arithmetic  2.75 us (2%)
  local copies, waits for them, and re-layouts  2.24 us (2%)
    pallas_call x1, Pallas kernels, body(): pl.pallas_call(_core_kernel, name='moe_core', out_shape=[sds((el, er, dm)...  79.3 us
    pallas_call x1, Pallas kernels, body(): pl.pallas_call(_grad_kernel, name='moe_grad', grid=(el // per,), out_shap...  35.5 us
    ppermute x3, starting transfers between devices, swap(): return lax.ppermute(a, ep, [(i, i ^ k) for i in range(n_src)])  3.51 us
  transfers between devices with their start and end apart: 3, of which 0 were waited for; matrix products, arithmetic and copies ran while one was open for 0% of the time, Pallas kernels for 29%

commit v1 on v0

v1 whole, which is shorter than its diff:
```python
import functools

import jax
import jax.numpy as jnp
from jax import lax
from jax.experimental import pallas as pl
from jax.experimental.pallas import tpu as pltpu
from jax.sharding import PartitionSpec as P

MESH = pl.DeviceIdType.MESH
F32 = jnp.float32
BF = jnp.bfloat16
ROWS = 16
SLOTS = 12
CORE_VMEM = 43
GRAD_VMEM = 14
GROUP = 2
DIM0 = (((0,), (0,)), ((), ()))
DIM1 = (((1,), (1,)), ((), ()))
ANY = pl.BlockSpec(memory_space=pl.ANY)


def _dot(a, b, dims=(((1,), (0,)), ((), ()))):
    return lax.dot_general(a, b, dims, preferred_element_type=F32)


def _core_kernel(x_hbm, dy_hbm, route_hbm, gate_hbm, w1_hbm, w3_hbm, w2_hbm,
                 xg, q, act, u, v, y_out, dg_out, dx0, dx1, dx2, dx3,
                 x_all, dy_all, route_all, gate_all, o, onehot, onehot_t, gate3_t,
                 w1, w3, w2, y_send, y_own, y_chip, y_far, d_own, dg_send, dg_all,
                 in_sem, w_sem, out_sem,
                 xs_sem, xr_sem, ys_sem, yr_sem, ts_sem, tr_sem, gts_sem, gtr_sem,
                 yc_s, yc_r, yf_s, yf_r, dc_s, dc_r, gs_sem, gr_sem):
    row, col, core = lax.axis_index('row'), lax.axis_index('col'), lax.axis_index('core')
    el, dm, fh = w1_hbm.shape
    td = x_hbm.shape[0]
    top = route_hbm.shape[0]
    n_src = x_all.shape[0]

    def peer(k):
        r = 1 - row if k & 4 else row
        c = 1 - col if k & 2 else col
        h = 1 - core if k & 1 else core
        return {'row': r, 'col': c, 'core': h}, r * 4 + c * 2 + h

    me = peer(0)[1]

    def start(copies):
        for c in copies:
            c.start()

    def wait(copies):
        for c in copies:
            c.wait()

    own = [pltpu.make_async_copy(a, b.at[me], in_sem.at[i])
           for i, (a, b) in enumerate(((route_hbm, route_all), (gate_hbm, gate_all), (x_hbm, x_all), (dy_hbm, dy_all)))]
    start(own)

    def up(e):
        slot = e % SLOTS
        return [pltpu.make_async_copy(a.at[e], b.at[slot], w_sem.at[j, slot])
                for j, (a, b) in enumerate(((w1_hbm, w1), (w3_hbm, w3)))]

    def down(e):
        return [pltpu.make_async_copy(w2_hbm.at[e], w2.at[e % SLOTS], w_sem.at[2, e % SLOTS])]

    barrier = pltpu.get_barrier_semaphore()
    for k in range(1, n_src):
        pl.semaphore_signal(barrier, inc=1, device_id=peer(k)[0], device_id_type=MESH)
    for e in range(SLOTS):
        start(up(e) + down(e))
    pl.semaphore_wait(barrier, n_src - 1)

    def send(src, dst, s_sem, r_sem, k):
        c = pltpu.make_async_remote_copy(src_ref=src, dst_ref=dst, send_sem=s_sem, recv_sem=r_sem,
                                         device_id=peer(k)[0], device_id_type=MESH)
        c.start()
        return c

    def arrive(dst, s_sem, r_sem):
        pltpu.make_async_remote_copy(src_ref=dst, dst_ref=dst, send_sem=s_sem, recv_sem=r_sem,
                                     device_id=peer(1)[0], device_id_type=MESH).wait_recv()

    sent = []
    wait(own[:2])
    for k in range(1, n_src):
        sent.append(send(route_all.at[me], route_all.at[me], ts_sem.at[k], tr_sem.at[me], k))
        sent.append(send(gate_all.at[me], gate_all.at[me], gts_sem.at[k], gtr_sem.at[me], k))
    wait(own[2:])
    for k in (2, 4, 6, 1):
        sent.append(send(x_all.at[me], x_all.at[me], xs_sem.at[k], xr_sem.at[me], k))

    for k in range(1, n_src):
        s = peer(k)[1]
        arrive(route_all.at[s], ts_sem.at[k], tr_sem.at[s])
        arrive(gate_all.at[s], gts_sem.at[k], gtr_sem.at[s])

    experts = lax.broadcasted_iota(jnp.int32, (el, td), 0) + me * el
    before = (lax.broadcasted_iota(jnp.int32, (td, td), 0) < lax.broadcasted_iota(jnp.int32, (td, td), 1))
    before = jnp.where(before, 1.0, 0.0).astype(BF)
    place = lax.broadcasted_iota(jnp.int32, (el, ROWS, td), 1).astype(F32)

    def gates_of(s):
        gate = jnp.zeros((el, td), F32)
        for j in range(top):
            gate = jnp.where(route_all[s, j:j + 1, :] == experts, gate_all[s, j:j + 1, :], gate)
        return gate

    def tables(s, _):
        hit = jnp.zeros((el, td), F32)
        for j in range(top):
            hit = jnp.where(route_all[s, j:j + 1, :] == experts, 1.0, hit)
        rank = jnp.where(hit > 0, _dot(hit.astype(BF), before), -1.0)
        sel = jnp.broadcast_to(rank[:, None, :], place.shape) == place
        hot = jnp.where(sel, 1.0, 0.0).reshape(el * ROWS, td)
        onehot[s] = hot.astype(BF)
        onehot_t[s] = hot.T.astype(BF)
        g = jnp.where(sel, jnp.broadcast_to(gates_of(s)[:, None, :], place.shape), 0.0)
        g = g.reshape(el * ROWS, td).T
        for i in range(3):
            part = g.astype(BF)
            gate3_t[s, i * td:(i + 1) * td, :] = part
            g = g - part.astype(F32)
        return 0

    lax.fori_loop(0, n_src, tables, 0)

    def rows_of(s):
        return pl.ds(pl.multiple_of(s * ROWS, ROWS), ROWS)

    for k in (0, 1, 2, 4, 6, 3, 5, 7):
        s = peer(k)[1]
        if k:
            arrive(x_all.at[s], xs_sem.at[k], xr_sem.at[s])
        if k in (2, 4, 6):
            sent.append(send(x_all.at[s], x_all.at[s], xs_sem.at[k + 1], xr_sem.at[s], 1))
        if k == 6:
            for j in (2, 4, 6, 1):
                sent.append(send(dy_all.at[me], dy_all.at[me], ys_sem.at[j], yr_sem.at[me], j))
        xg[:, rows_of(s), :] = _dot(onehot[s], x_all[s]).astype(BF).reshape(el, ROWS, dm)

    def group(p):
        return [p * GROUP + i for i in range(GROUP)]

    groups = el // GROUP

    def forward_hidden(e):
        slot = e % SLOTS
        xe = xg[e]
        ue = _dot(xe, w1[slot]).astype(BF)
        ve = _dot(xe, w3[slot]).astype(BF)
        u[e] = ue
        v[e] = ve
        uf = ue.astype(F32)
        act[e] = (uf * jax.nn.sigmoid(uf) * ve.astype(F32)).astype(BF)

    def forward_out(e):
        o[e] = _dot(act[e], w2[e % SLOTS]).astype(BF)

    def ahead(copies, es):
        for e in es:
            @pl.when(e + SLOTS < el)
            def _():
                start(copies(e + SLOTS))

    def forward(p, _):
        prev, now = group(p - 1), group(p)
        for e in prev:
            wait(down(e))
        for e in now:
            wait(up(e))
        for e in prev:
            forward_out(e)
        for e in now:
            forward_hidden(e)
        ahead(down, prev)
        ahead(up, now)
        return 0

    for e in group(0):
        wait(up(e))
    for e in group(0):
        forward_hidden(e)
    for e in group(0):
        start(up(e + SLOTS))
    lax.fori_loop(1, groups, forward, 0)
    for e in group(groups - 1):
        wait(down(e))
    for e in group(groups - 1):
        forward_out(e)

    def y_part(s):
        z = _dot(gate3_t[s], o[:, rows_of(s), :].reshape(el * ROWS, dm))
        return z[:td] + z[td:2 * td] + z[2 * td:]

    chip = []
    for j in range(4):
        y_send[j] = y_part(peer(2 * j + 1)[1])
        chip.append(send(y_send.at[j], y_chip.at[j], yc_s.at[j], yc_r.at[j], 1))
    for k in (2, 4, 6):
        s = peer(k)[1]
        arrive(dy_all.at[s], ys_sem.at[k], yr_sem.at[s])
        sent.append(send(dy_all.at[s], dy_all.at[s], ys_sem.at[k + 1], yr_sem.at[s], 1))
    for j in range(4):
        y_own[j] = y_part(peer(2 * j)[1])
    for j in (3, 1, 2, 0):
        arrive(y_chip.at[j], yc_s.at[j], yc_r.at[j])
        y_own[j] = y_own[j] + y_chip[j]
        if j:
            sent.append(send(y_own.at[j], y_far.at[j - 1], yf_s.at[j - 1], yf_r.at[j - 1], 2 * j))

    def dispatch_dy(s):
        gate = gates_of(s)
        dgt = []
        part = el // 4
        for h in range(4):
            es = slice(h * part, (h + 1) * part)
            hot = onehot[s, h * part * ROWS:(h + 1) * part * ROWS, :]
            d = _dot(hot, dy_all[s])
            hot = hot.astype(F32)
            os = o[es, rows_of(s), :].reshape(part * ROWS, dm).astype(F32)
            dg = jnp.sum(d * os, axis=1, keepdims=True)
            dgt.append(jnp.sum((hot * dg).reshape(part, ROWS, td), axis=1))
            g = jnp.broadcast_to(gate[es][:, None, :], (part, ROWS, td)).reshape(part * ROWS, td)
            g = jnp.sum(hot * g, axis=1, keepdims=True)
            q[es, rows_of(s), :] = (g * d).astype(BF).reshape(part, ROWS, dm)
        dgt = jnp.concatenate(dgt, axis=0)
        for j in range(top):
            m = route_all[s, j:j + 1, :] == experts
            dg_send[s, j:j + 1, :] = jnp.sum(jnp.where(m, dgt, 0.0), axis=0, keepdims=True)

    for k in (0, 1, 2, 4, 6, 3, 5, 7):
        s = peer(k)[1]
        if k in (1, 3, 5, 7):
            arrive(dy_all.at[s], ys_sem.at[k], yr_sem.at[s])
        dispatch_dy(s)
        if k:
            sent.append(send(dg_send.at[s], dg_all.at[me], gs_sem.at[k], gr_sem.at[me], k))
        else:
            dg_all[me] = dg_send[s]

    def backward_hidden(e):
        da = _dot(q[e], w2[e % SLOTS], DIM1).astype(BF).astype(F32)
        uf = u[e].astype(F32)
        vf = v[e].astype(F32)
        sg = jax.nn.sigmoid(uf)
        u[e] = (da * vf * sg * (1 + uf * (1 - sg))).astype(BF)
        v[e] = (da * (uf * sg)).astype(BF)

    def backward_out(e):
        slot = e % SLOTS
        o[e] = (_dot(u[e], w1[slot], DIM1) + _dot(v[e], w3[slot], DIM1)).astype(BF)

    def refill(copies, es):
        for e in es:
            @pl.when(e >= SLOTS)
            def _():
                start(copies(e - SLOTS))

    def ready(copies, es):
        for e in es:
            @pl.when(e < el - SLOTS)
            def _():
                wait(copies(e))

    def down_group(p):
        return [el - 1 - (p * GROUP + i) for i in range(GROUP)]

    def backward(p, _):
        prev, now = down_group(p - 1), down_group(p)
        ready(up, prev)
        ready(down, now)
        for e in prev:
            backward_out(e)
        for e in now:
            backward_hidden(e)
        refill(up, prev)
        refill(down, now)
        return 0

    for e in down_group(0):
        backward_hidden(e)
    refill(down, down_group(0))
    lax.fori_loop(1, groups, backward, 0)
    ready(up, down_group(groups - 1))
    for e in down_group(groups - 1):
        backward_out(e)

    for k in range(1, n_src):
        s = peer(k)[1]
        arrive(dg_all.at[s], gs_sem.at[k], gr_sem.at[s])
    for c in chip:
        c.wait_send()

    def dx_part(s):
        return _dot(onehot_t[s], o[:, rows_of(s), :].reshape(el * ROWS, dm))

    for j in range(4):
        y_send[j] = dx_part(peer(2 * j + 1)[1])
        sent.append(send(y_send.at[j], y_chip.at[j], dc_s.at[j], dc_r.at[j], 1))
    for j in range(4):
        d_own[j] = dx_part(peer(2 * j)[1])
    outs = []
    for j, out in ((3, dx3), (1, dx1), (2, dx2), (0, dx0)):
        arrive(y_chip.at[j], dc_s.at[j], dc_r.at[j])
        d_own[j] = d_own[j] + y_chip[j]
        outs.append(pltpu.make_async_copy(d_own.at[j], out, out_sem.at[j]))
        outs[-1].start()

    for j in range(3):
        arrive(y_far.at[j], yf_s.at[j], yf_r.at[j])
    y_out[...] = (y_own[0] + y_far[0] + y_far[1] + y_far[2]).astype(BF)
    dg_out[...] = jnp.sum(dg_all[...], axis=0)

    for c in sent:
        c.wait_send()
    wait(outs)


def _grad_kernel(xg, q, act, du, dv, y, dg, dw1, dw3, dw2, y_out, dg_out):
    for i in range(xg.shape[0]):
        dw1[i] = _dot(xg[i], du[i], DIM0)
        dw3[i] = _dot(xg[i], dv[i], DIM0)
        dw2[i] = _dot(act[i], q[i], DIM0)
    y_out[...] = y[...]
    dg_out[...] = dg[...]


def solution(mesh):
    ep = ('row', 'col', 'core')
    n_src = mesh.shape['row'] * mesh.shape['col'] * mesh.shape['core']
    tspec = P(('dp',) + ep, None)
    wspec = P(ep, None, None)
    gspec = P(('dp',) + ep, None, None)

    def body(x, route_idx, gates, w1, w3, w2, dy):
        td, top = route_idx.shape
        el, dm, fh = w1.shape
        er = n_src * ROWS
        sds = jax.ShapeDtypeStruct
        vmem = pltpu.VMEM
        dma = pltpu.SemaphoreType.DMA
        block = (td, dm)
        small = (n_src, top, td)
        whole = pl.BlockSpec(memory_space=pltpu.VMEM)
        flops = 2 * el * er * dm * fh * 6
        xg, q, act, du, dv, y, dg, dx0, dx1, dx2, dx3 = pl.pallas_call(
            _core_kernel,
            name='moe_core',
            out_shape=[vmem((el, er, dm), BF), vmem((el, er, dm), BF)] + [vmem((el, er, fh), BF)] * 3
            + [vmem(block, BF), vmem((top, td), F32)] + [sds(block, F32)] * 4,
            in_specs=[ANY] * 7,
            out_specs=[whole] * 7 + [ANY] * 4,
            scratch_shapes=[
                vmem((n_src,) + block, BF), vmem((n_src,) + block, BF), vmem(small, jnp.int32), vmem(small, F32),
                vmem((el, er, dm), BF),
                vmem((n_src, el * ROWS, td), BF), vmem((n_src, td, el * ROWS), BF), vmem((n_src, 3 * td, el * ROWS), BF),
                vmem((SLOTS, dm, fh), BF), vmem((SLOTS, dm, fh), BF), vmem((SLOTS, fh, dm), BF),
                vmem((4,) + block, F32), vmem((4,) + block, F32), vmem((4,) + block, F32), vmem((3,) + block, F32),
                vmem((4,) + block, F32), vmem(small, F32), vmem(small, F32),
                dma((4,)), dma((3, SLOTS)), dma((4,)),
                dma((8,)), dma((8,)), dma((8,)), dma((8,)), dma((8,)), dma((8,)), dma((8,)), dma((8,)),
                dma((4,)), dma((4,)), dma((3,)), dma((3,)), dma((4,)), dma((4,)), dma((8,)), dma((8,)),
            ],
            compiler_params=pltpu.CompilerParams(collective_id=0, has_side_effects=True, vmem_limit_bytes=CORE_VMEM << 20),
            cost_estimate=pl.CostEstimate(flops=flops, bytes_accessed=88 << 20, transcendentals=0),
        )(x, dy, route_idx.T, gates.T, w1, w3, w2)

        def swap(a, k):
            return lax.ppermute(a, ep, [(i, i ^ k) for i in range(n_src)])

        far = [swap(dx3, 6), swap(dx1, 2), swap(dx2, 4)]
        per = 2
        spec = lambda a, b: pl.BlockSpec((per, a, b), lambda i: (i, 0, 0))
        once = lambda a, b: pl.BlockSpec((a, b), lambda i: (0, 0))

        dw1, dw3, dw2, y, dg = pl.pallas_call(
            _grad_kernel,
            name='moe_grad',
            grid=(el // per,),
            out_shape=[sds((el, dm, fh), F32), sds((el, dm, fh), F32), sds((el, fh, dm), F32), sds(block, BF), sds((top, td), F32)],
            in_specs=[spec(er, dm), spec(er, dm), spec(er, fh), spec(er, fh), spec(er, fh), once(td, dm), once(top, td)],
            out_specs=[spec(dm, fh), spec(dm, fh), spec(fh, dm), once(td, dm), once(top, td)],
            compiler_params=pltpu.CompilerParams(vmem_limit_bytes=GRAD_VMEM << 20),
            cost_estimate=pl.CostEstimate(flops=2 * el * er * dm * fh * 3, bytes_accessed=90 << 20, transcendentals=0),
        )(xg, q, act, du, dv, y, dg)
        dx = (dx0 + far[0] + far[1] + far[2]).astype(BF)
        return y, dx, dg.T, dw1, dw3, dw2

    return jax.shard_map(body, mesh=mesh, in_specs=(tspec, tspec, tspec, wspec, wspec, wspec, tspec),
                         out_specs=(tspec, tspec, tspec, gspec, gspec, gspec), check_vma=False)
```

time: 125 us -> 96 us (0.77)
  Pallas kernels: 115 us -> 90.9 us
  local copies, waits for them, and re-layouts: 2.24 us -> 0.01 us
  other arithmetic: 2.75 us -> 0.77 us
    pallas_call x1, Pallas kernels: 79.3 us -> 62.7 us  [body(): pl.pallas_call(_core_kernel, name='moe_core', out_shape=[vmem((el, er, dm...]
    pallas_call x1, Pallas kernels: 35.5 us -> 28.2 us  [body(): pl.pallas_call(_grad_kernel, name='moe_grad', grid=(el // per,), out_shap...]
    unnamed x6 -> x2, local copies, waits for them, and re-layouts: 2.24 us -> 0.01 us
    concatenate x1 -> x0, other arithmetic: 1.29 us -> none  [body(): tab = jnp.concatenate([route_idx.T.astype(F32), gates.T], axis=0)]
where the time goes in v1:
time: 96 us; the launch traced here: 95.9 us
  Pallas kernels  90.9 us (95%)
  starting transfers between devices  3.51 us (4%)
    pallas_call x1, Pallas kernels, body(): pl.pallas_call(_core_kernel, name='moe_core', out_shape=[vmem((el, er, dm...  62.7 us
    pallas_call x1, Pallas kernels, body(): pl.pallas_call(_grad_kernel, name='moe_grad', grid=(el // per,), out_shap...  28.2 us
    ppermute x3, starting transfers between devices, swap(): return lax.ppermute(a, ep, [(i, i ^ k) for i in range(n_src)])  3.51 us
  transfers between devices with their start and end apart: 3, of which 0 were waited for; matrix products, arithmetic and copies ran while one was open for 0% of the time, Pallas kernels for 29%

profile of v1, /device:TPU:0, one launch (start us, length us, event | category | flops | bytes accessed | tf_op | source)
XLA Modules:
  0.0 95.9 jit_solution(9777643186392129106)
XLA Ops:
  0.6 62.7 %moe_core.1 = (bf16[32,128,896]{2,1,0:T(8,128)(2,1)S(1)}, bf16[32,128,896]{2,1,0:T(8,128)(2,1)S(1)}, bf16[32,128,256]{2,1,0:T(8,128)(2,1)S(1)}, bf16[32,128,256]...) custom-call(bf16[128,896]{1,0:T(8,128)(2,1)} %x_hbm.1, ...), custom_call_target="tpu_custom_call" | custom-call | flops 11274289152 | bytes 92274688 | tf_op jit(solution)/shard_map/moe_core/pallas_call | solution.py:348
  63.4 0.0 copy-start
  63.4 1.8 %collective-permute-start = (f32[128,896]{1,0:T(8,128)}, f32[128,896]{1,0:T(8,128)S(1)}, u32[]{:S(2)}, u32[]{:S(2)}) collective-permute-start(f32[128,896]{1,0:T(8,128)} %get-tuple-element.31), channel_id=1, source_target_pairs={{0,6},{1,7},{2,4},{3,5},{4,2},{5,3},{6,0},{7,1}} | collective-permute-start | bytes 1376264 | tf_op jit(solution)/shard_map/ppermute | solution.py:371
  65.2 0.6 collective-permute-start.1
  65.8 1.1 %collective-permute-start.2 = (f32[128,896]{1,0:T(8,128)}, f32[128,896]{1,0:T(8,128)S(1)}, u32[]{:S(2)}, u32[]{:S(2)}) collective-permute-start(f32[128,896]{1,0:T(8,128)} %get-tuple-element.33), channel_id=1, source_target_pairs={{0,4},{1,5},{2,6},{3,7},{4,0},{5,1},{6,2},{7,3}} | collective-permute-start | bytes 1376264 | tf_op jit(solution)/shard_map/ppermute | solution.py:371
  66.9 28.2 %moe_grad.1 = (f32[32,896,256]{2,1,0:T(8,128)}, f32[32,896,256]{2,1,0:T(8,128)}, f32[32,256,896]{2,1,0:T(8,128)}, bf16[128,896]{1,0:T(8,128)(2,1)}, f32[8,128]{1,0:T(8,128)}) custom-call(bf16[32,128,896]{2,1,0:T(8,128)(2,1)S(1)} %get-tuple-element.22.xg, bf16[32,128,896]{2,1,0:T(8,128)(2,1)S(1)} %get-tuple-element.23.q, ...), custom_call_target="tpu_custom_call" | custom-call | flops 5637144576 | bytes 94371840 | tf_op jit(solution)/shard_map/moe_grad/pallas_call | solution.py:378
  95.1 0.0 collective-permute-done
  95.1 0.0 collective-permute-done.1
  95.1 0.0 collective-permute-done.2
  95.1 0.0 copy-done
  95.1 0.8 add_convert_fusion
Async XLA Ops:
  63.4 31.7 %copy-start = (f32[128,896]{1,0:T(8,128)S(1)}, f32[128,896]{1,0:T(8,128)}, u32[]{:S(2)}) copy-start(f32[128,896]{1,0:T(8,128)} %get-tuple-element.30) | copy-start | bytes 1376260
  63.4 31.7 %collective-permute-start = (f32[128,896]{1,0:T(8,128)}, f32[128,896]{1,0:T(8,128)S(1)}, u32[]{:S(2)}, u32[]{:S(2)}) collective-permute-start(f32[128,896]{1,0:T(8,128)} %get-tuple-element.31), channel_id=1, source_target_pairs={{0,6},{1,7},{2,4},{3,5},{4,2},{5,3},{6,0},{7,1}} | collective-permute-start | bytes 1376264 | tf_op jit(solution)/shard_map/ppermute | solution.py:371
  65.2 29.9 %collective-permute-start.1 = (f32[128,896]{1,0:T(8,128)}, f32[128,896]{1,0:T(8,128)S(1)}, u32[]{:S(2)}, u32[]{:S(2)}) collective-permute-start(f32[128,896]{1,0:T(8,128)} %get-tuple-element.32), channel_id=1, source_target_pairs={{0,2},{1,3},{2,0},{3,1},{4,6},{5,7},{6,4},{7,5}} | collective-permute-start | bytes 1376264 | tf_op jit(solution)/shard_map/ppermute | solution.py:371
  65.8 29.4 %collective-permute-start.2 = (f32[128,896]{1,0:T(8,128)}, f32[128,896]{1,0:T(8,128)S(1)}, u32[]{:S(2)}, u32[]{:S(2)}) collective-permute-start(f32[128,896]{1,0:T(8,128)} %get-tuple-element.33), channel_id=1, source_target_pairs={{0,4},{1,5},{2,6},{3,7},{4,0},{5,1},{6,2},{7,3}} | collective-permute-start | bytes 1376264 | tf_op jit(solution)/shard_map/ppermute | solution.py:371

commit v2 on v1

--- a/solution.py
+++ b/solution.py
@@ -12,9 +12,10 @@
 BF = jnp.bfloat16
 ROWS = 16
 SLOTS = 12
+FORWARD_AT = 4
 CORE_VMEM = 43
 GRAD_VMEM = 14
-GROUP = 2
+GROUP = 4
 DIM0 = (((0,), (0,)), ((), ()))
 DIM1 = (((1,), (1,)), ((), ()))
 ANY = pl.BlockSpec(memory_space=pl.ANY)
@@ -88,8 +89,24 @@
         sent.append(send(route_all.at[me], route_all.at[me], ts_sem.at[k], tr_sem.at[me], k))
         sent.append(send(gate_all.at[me], gate_all.at[me], gts_sem.at[k], gtr_sem.at[me], k))
     wait(own[2:])
-    for k in (2, 4, 6, 1):
-        sent.append(send(x_all.at[me], x_all.at[me], xs_sem.at[k], xr_sem.at[me], k))
+    half = td // 2
+
+    def x_half(s, h):
+        return x_all.at[s, pl.ds(h * half, half)]
+
+    def x_send(s, h, k):
+        i = len(x_sent)
+        x_sent.append(send(x_half(s, h), x_half(s, h), xs_sem.at[i], xr_sem.at[2 * s + h], k))
+
+    def x_wait(s, h):
+        arrive(x_half(s, h), xs_sem.at[0], xr_sem.at[2 * s + h])
+
+    x_sent = []
+    for h in range(2):
+        x_send(me, h, 2)
+        x_send(me, 1 - h, 4)
+    for h in range(2):
+        x_send(me, h, 1)
 
     for k in range(1, n_src):
         s = peer(k)[1]
@@ -129,16 +146,41 @@
     def rows_of(s):
         return pl.ds(pl.multiple_of(s * ROWS, ROWS), ROWS)
 
-    for k in (0, 1, 2, 4, 6, 3, 5, 7):
+    def dispatch_x(k):
         s = peer(k)[1]
-        if k:
-            arrive(x_all.at[s], xs_sem.at[k], xr_sem.at[s])
-        if k in (2, 4, 6):
-            sent.append(send(x_all.at[s], x_all.at[s], xs_sem.at[k + 1], xr_sem.at[s], 1))
-        if k == 6:
-            for j in (2, 4, 6, 1):
-                sent.append(send(dy_all.at[me], dy_all.at[me], ys_sem.at[j], yr_sem.at[me], j))
         xg[:, rows_of(s), :] = _dot(onehot[s], x_all[s]).astype(BF).reshape(el, ROWS, dm)
+
+    dispatch_x(0)
+    near_x, near_y, diagonal = peer(2)[1], peer(4)[1], peer(6)[1]
+    x_wait(near_x, 0)
+    x_send(near_x, 0, 4)
+    x_send(near_x, 0, 1)
+    x_wait(near_y, 1)
+    x_send(near_y, 1, 2)
+    x_send(near_y, 1, 1)
+    for h in range(2):
+        x_wait(peer(1)[1], h)
+    dispatch_x(1)
+    x_wait(near_x, 1)
+    x_send(near_x, 1, 1)
+    x_wait(near_y, 0)
+    x_send(near_y, 0, 1)
+    for k in (2, 4):
+        dispatch_x(k)
+    for k in (3, 5):
+        for h in range(2):
+            x_wait(peer(k)[1], h)
+        dispatch_x(k)
+    for h in range(2):
+        x_wait(diagonal, h)
+        x_send(diagonal, h, 1)
+    for k in (2, 4, 6, 1):
+        sent.append(send(dy_all.at[me], dy_all.at[me], ys_sem.at[k], yr_sem.at[me], k))
+    dispatch_x(6)
+    for h in range(2):
+        x_wait(peer(7)[1], h)
+    dispatch_x(7)
+    sent += x_sent
 
     def group(p):
         return [p * GROUP + i for i in range(GROUP)]
@@ -194,6 +236,24 @@
         z = _dot(gate3_t[s], o[:, rows_of(s), :].reshape(el * ROWS, dm))
         return z[:td] + z[td:2 * td] + z[2 * td:]
 
+    def y_half(j, h):
+        return y_own.at[j, pl.ds(h * half, half)]
+
+    def far_send(j, h, i, k):
+        sent.append(send(y_half(j, h), y_far.at[i], yf_s.at[i], yf_r.at[i], k))
+
+    def far_add(i, j, h):
+        arrive(y_far.at[i], yf_s.at[i], yf_r.at[i])
+        y_half(j, h)[...] = y_half(j, h)[...] + y_far[i]
+
+    def far_forward():
+        far_add(0, 2, 0)
+        far_send(2, 0, 4, 4)
+        far_add(1, 1, 1)
+        far_send(1, 1, 5, 2)
+        far_add(2, 0, 0)
+        far_add(3, 0, 1)
+
     chip = []
     for j in range(4):
         y_send[j] = y_part(peer(2 * j + 1)[1])
@@ -207,8 +267,11 @@
     for j in (3, 1, 2, 0):
         arrive(y_chip.at[j], yc_s.at[j], yc_r.at[j])
         y_own[j] = y_own[j] + y_chip[j]
-        if j:
-            sent.append(send(y_own.at[j], y_far.at[j - 1], yf_s.at[j - 1], yf_r.at[j - 1], 2 * j))
+        if j == 2:
+            far_send(3, 0, 0, 2)
+            far_send(3, 1, 1, 4)
+            far_send(1, 0, 2, 2)
+            far_send(2, 1, 3, 4)
 
     def dispatch_dy(s):
         gate = gates_of(s)
@@ -282,7 +345,9 @@
     for e in down_group(0):
         backward_hidden(e)
     refill(down, down_group(0))
-    lax.fori_loop(1, groups, backward, 0)
+    lax.fori_loop(1, FORWARD_AT, backward, 0)
+    far_forward()
+    lax.fori_loop(FORWARD_AT, groups, backward, 0)
     ready(up, down_group(groups - 1))
     for e in down_group(groups - 1):
         backward_out(e)
@@ -301,17 +366,17 @@
         sent.append(send(y_send.at[j], y_chip.at[j], dc_s.at[j], dc_r.at[j], 1))
     for j in range(4):
         d_own[j] = dx_part(peer(2 * j)[1])
+    for i, h in ((4, 0), (5, 1)):
+        far_add(i, 0, h)
+    y_out[...] = y_own[0].astype(BF)
+    dg_out[...] = jnp.sum(dg_all[...], axis=0)
+
     outs = []
     for j, out in ((3, dx3), (1, dx1), (2, dx2), (0, dx0)):
         arrive(y_chip.at[j], dc_s.at[j], dc_r.at[j])
         d_own[j] = d_own[j] + y_chip[j]
         outs.append(pltpu.make_async_copy(d_own.at[j], out, out_sem.at[j]))
         outs[-1].start()
-
-    for j in range(3):
-        arrive(y_far.at[j], yf_s.at[j], yf_r.at[j])
-    y_out[...] = (y_own[0] + y_far[0] + y_far[1] + y_far[2]).astype(BF)
-    dg_out[...] = jnp.sum(dg_all[...], axis=0)
 
     for c in sent:
         c.wait_send()
@@ -357,11 +422,11 @@
                 vmem((el, er, dm), BF),
                 vmem((n_src, el * ROWS, td), BF), vmem((n_src, td, el * ROWS), BF), vmem((n_src, 3 * td, el * ROWS), BF),
                 vmem((SLOTS, dm, fh), BF), vmem((SLOTS, dm, fh), BF), vmem((SLOTS, fh, dm), BF),
-                vmem((4,) + block, F32), vmem((4,) + block, F32), vmem((4,) + block, F32), vmem((3,) + block, F32),
+                vmem((4,) + block, F32), vmem((4,) + block, F32), vmem((4,) + block, F32), vmem((6, td // 2, dm), F32),
                 vmem((4,) + block, F32), vmem(small, F32), vmem(small, F32),
                 dma((4,)), dma((3, SLOTS)), dma((4,)),
-                dma((8,)), dma((8,)), dma((8,)), dma((8,)), dma((8,)), dma((8,)), dma((8,)), dma((8,)),
-                dma((4,)), dma((4,)), dma((3,)), dma((3,)), dma((4,)), dma((4,)), dma((8,)), dma((8,)),
+                dma((16,)), dma((16,)), dma((8,)), dma((8,)), dma((8,)), dma((8,)), dma((8,)), dma((8,)),
+                dma((4,)), dma((4,)), dma((6,)), dma((6,)), dma((4,)), dma((4,)), dma((8,)), dma((8,)),
             ],
             compiler_params=pltpu.CompilerParams(collective_id=0, has_side_effects=True, vmem_limit_bytes=CORE_VMEM << 20),
             cost_estimate=pl.CostEstimate(flops=flops, bytes_accessed=88 << 20, transcendentals=0),

time: 96 us -> 92.4 us (0.963)
  Pallas kernels: 90.9 us -> 87.4 us
    pallas_call x1, Pallas kernels: 62.7 us -> 59.2 us  [body(): pl.pallas_call(_core_kernel, name='moe_core', out_shape=[vmem((el, er, dm...]
  transfers between devices with their start and end apart: 3 -> 3, of which waited for: 0 -> 0; matrix products, arithmetic and copies ran while one was open for 0% -> 0% of each run, Pallas kernels for 29% -> 31%
where the time goes in v2:
time: 92.4 us; the launch traced here: 92.3 us
  Pallas kernels  87.4 us (95%)
  starting transfers between devices  3.51 us (4%)
    pallas_call x1, Pallas kernels, body(): pl.pallas_call(_core_kernel, name='moe_core', out_shape=[vmem((el, er, dm...  59.2 us
    pallas_call x1, Pallas kernels, body(): pl.pallas_call(_grad_kernel, name='moe_grad', grid=(el // per,), out_shap...  28.2 us
    ppermute x3, starting transfers between devices, swap(): return lax.ppermute(a, ep, [(i, i ^ k) for i in range(n_src)])  3.51 us
  transfers between devices with their start and end apart: 3, of which 0 were waited for; matrix products, arithmetic and copies ran while one was open for 0% of the time, Pallas kernels for 31%

profile of v2, /device:TPU:0, one launch (start us, length us, event | category | flops | bytes accessed | tf_op | source)
XLA Modules:
  0.0 92.3 jit_solution(12136907723343248008)
XLA Ops:
  0.6 59.2 %moe_core.1 = (bf16[32,128,896]{2,1,0:T(8,128)(2,1)S(1)}, bf16[32,128,896]{2,1,0:T(8,128)(2,1)S(1)}, bf16[32,128,256]{2,1,0:T(8,128)(2,1)S(1)}, bf16[32,128,256]...) custom-call(bf16[128,896]{1,0:T(8,128)(2,1)} %x_hbm.1, ...), custom_call_target="tpu_custom_call" | custom-call | flops 11274289152 | bytes 92274688 | tf_op jit(solution)/shard_map/moe_core/pallas_call | solution.py:413
  59.8 0.0 copy-start
  59.8 1.5 %collective-permute-start = (f32[128,896]{1,0:T(8,128)}, f32[128,896]{1,0:T(8,128)S(1)}, u32[]{:S(2)}, u32[]{:S(2)}) collective-permute-start(f32[128,896]{1,0:T(8,128)} %get-tuple-element.31), channel_id=1, source_target_pairs={{0,6},{1,7},{2,4},{3,5},{4,2},{5,3},{6,0},{7,1}} | collective-permute-start | bytes 1376264 | tf_op jit(solution)/shard_map/ppermute | solution.py:436
  61.3 1.1 %collective-permute-start.1 = (f32[128,896]{1,0:T(8,128)}, f32[128,896]{1,0:T(8,128)S(1)}, u32[]{:S(2)}, u32[]{:S(2)}) collective-permute-start(f32[128,896]{1,0:T(8,128)} %get-tuple-element.32), channel_id=1, source_target_pairs={{0,2},{1,3},{2,0},{3,1},{4,6},{5,7},{6,4},{7,5}} | collective-permute-start | bytes 1376264 | tf_op jit(solution)/shard_map/ppermute | solution.py:436
  62.4 1.0 %collective-permute-start.2 = (f32[128,896]{1,0:T(8,128)}, f32[128,896]{1,0:T(8,128)S(1)}, u32[]{:S(2)}, u32[]{:S(2)}) collective-permute-start(f32[128,896]{1,0:T(8,128)} %get-tuple-element.33), channel_id=1, source_target_pairs={{0,4},{1,5},{2,6},{3,7},{4,0},{5,1},{6,2},{7,3}} | collective-permute-start | bytes 1376264 | tf_op jit(solution)/shard_map/ppermute | solution.py:436
  63.3 28.2 %moe_grad.1 = (f32[32,896,256]{2,1,0:T(8,128)}, f32[32,896,256]{2,1,0:T(8,128)}, f32[32,256,896]{2,1,0:T(8,128)}, bf16[128,896]{1,0:T(8,128)(2,1)}, f32[8,128]{1,0:T(8,128)}) custom-call(bf16[32,128,896]{2,1,0:T(8,128)(2,1)S(1)} %get-tuple-element.22.xg, bf16[32,128,896]{2,1,0:T(8,128)(2,1)S(1)} %get-tuple-element.23.q, ...), custom_call_target="tpu_custom_call" | custom-call | flops 5637144576 | bytes 94371840 | tf_op jit(solution)/shard_map/moe_grad/pallas_call | solution.py:443
  91.5 0.0 collective-permute-done
  91.5 0.0 collective-permute-done.1
  91.5 0.0 collective-permute-done.2
  91.6 0.0 copy-done
  91.6 0.8 add_convert_fusion
Async XLA Ops:
  59.8 31.7 %copy-start = (f32[128,896]{1,0:T(8,128)S(1)}, f32[128,896]{1,0:T(8,128)}, u32[]{:S(2)}) copy-start(f32[128,896]{1,0:T(8,128)} %get-tuple-element.30) | copy-start | bytes 1376260
  59.8 31.7 %collective-permute-start = (f32[128,896]{1,0:T(8,128)}, f32[128,896]{1,0:T(8,128)S(1)}, u32[]{:S(2)}, u32[]{:S(2)}) collective-permute-start(f32[128,896]{1,0:T(8,128)} %get-tuple-element.31), channel_id=1, source_target_pairs={{0,6},{1,7},{2,4},{3,5},{4,2},{5,3},{6,0},{7,1}} | collective-permute-start | bytes 1376264 | tf_op jit(solution)/shard_map/ppermute | solution.py:436
  61.3 30.3 %collective-permute-start.1 = (f32[128,896]{1,0:T(8,128)}, f32[128,896]{1,0:T(8,128)S(1)}, u32[]{:S(2)}, u32[]{:S(2)}) collective-permute-start(f32[128,896]{1,0:T(8,128)} %get-tuple-element.32), channel_id=1, source_target_pairs={{0,2},{1,3},{2,0},{3,1},{4,6},{5,7},{6,4},{7,5}} | collective-permute-start | bytes 1376264 | tf_op jit(solution)/shard_map/ppermute | solution.py:436
  62.4 29.2 %collective-permute-start.2 = (f32[128,896]{1,0:T(8,128)}, f32[128,896]{1,0:T(8,128)S(1)}, u32[]{:S(2)}, u32[]{:S(2)}) collective-permute-start(f32[128,896]{1,0:T(8,128)} %get-tuple-element.33), channel_id=1, source_target_pairs={{0,4},{1,5},{2,6},{3,7},{4,0},{5,1},{6,2},{7,3}} | collective-permute-start | bytes 1376264 | tf_op jit(solution)/shard_map/ppermute | solution.py:436

commit v3 on v2

--- a/solution.py
+++ b/solution.py
@@ -12,8 +12,7 @@
 BF = jnp.bfloat16
 ROWS = 16
 SLOTS = 12
-FORWARD_AT = 4
-CORE_VMEM = 43
+CORE_VMEM = 41
 GRAD_VMEM = 14
 GROUP = 4
 DIM0 = (((0,), (0,)), ((), ()))
@@ -26,10 +25,10 @@
 
 
 def _core_kernel(x_hbm, dy_hbm, route_hbm, gate_hbm, w1_hbm, w3_hbm, w2_hbm,
-                 xg, q, act, u, v, y_out, dg_out, dx0, dx1, dx2, dx3,
+                 xg, q, act, u, v, dg_out, y_here, dx_here, to_x, to_y, to_xy,
                  x_all, dy_all, route_all, gate_all, o, onehot, onehot_t, gate3_t,
-                 w1, w3, w2, y_send, y_own, y_chip, y_far, d_own, dg_send, dg_all,
-                 in_sem, w_sem, out_sem,
+                 w1, w3, w2, y_send, y_own, y_chip, y_far, dg_send, dg_all,
+                 in_sem, w_sem,
                  xs_sem, xr_sem, ys_sem, yr_sem, ts_sem, tr_sem, gts_sem, gtr_sem,
                  yc_s, yc_r, yf_s, yf_r, dc_s, dc_r, gs_sem, gr_sem):
     row, col, core = lax.axis_index('row'), lax.axis_index('col'), lax.axis_index('core')
@@ -242,17 +241,9 @@
     def far_send(j, h, i, k):
         sent.append(send(y_half(j, h), y_far.at[i], yf_s.at[i], yf_r.at[i], k))
 
-    def far_add(i, j, h):
+    def far_sum(i, j, h):
         arrive(y_far.at[i], yf_s.at[i], yf_r.at[i])
-        y_half(j, h)[...] = y_half(j, h)[...] + y_far[i]
-
-    def far_forward():
-        far_add(0, 2, 0)
-        far_send(2, 0, 4, 4)
-        far_add(1, 1, 1)
-        far_send(1, 1, 5, 2)
-        far_add(2, 0, 0)
-        far_add(3, 0, 1)
+        return y_half(j, h)[...] + y_far[i]
 
     chip = []
     for j in range(4):
@@ -345,9 +336,7 @@
     for e in down_group(0):
         backward_hidden(e)
     refill(down, down_group(0))
-    lax.fori_loop(1, FORWARD_AT, backward, 0)
-    far_forward()
-    lax.fori_loop(FORWARD_AT, groups, backward, 0)
+    lax.fori_loop(1, groups, backward, 0)
     ready(up, down_group(groups - 1))
     for e in down_group(groups - 1):
         backward_out(e)
@@ -364,31 +353,29 @@
     for j in range(4):
         y_send[j] = dx_part(peer(2 * j + 1)[1])
         sent.append(send(y_send.at[j], y_chip.at[j], dc_s.at[j], dc_r.at[j], 1))
+    d_own = (dx_here, to_x.at[pl.ds(0, td)], to_y.at[pl.ds(0, td)], to_xy)
     for j in range(4):
-        d_own[j] = dx_part(peer(2 * j)[1])
-    for i, h in ((4, 0), (5, 1)):
-        far_add(i, 0, h)
-    y_out[...] = y_own[0].astype(BF)
+        d_own[j][...] = dx_part(peer(2 * j)[1])
+
+    to_y[pl.ds(td, half), :] = far_sum(0, 2, 0)
+    to_x[pl.ds(td, half), :] = far_sum(1, 1, 1)
+    y_here[pl.ds(0, half), :] = far_sum(2, 0, 0)
+    y_here[pl.ds(half, half), :] = far_sum(3, 0, 1)
     dg_out[...] = jnp.sum(dg_all[...], axis=0)
 
-    outs = []
-    for j, out in ((3, dx3), (1, dx1), (2, dx2), (0, dx0)):
+    for j in range(4):
         arrive(y_chip.at[j], dc_s.at[j], dc_r.at[j])
-        d_own[j] = d_own[j] + y_chip[j]
-        outs.append(pltpu.make_async_copy(d_own.at[j], out, out_sem.at[j]))
-        outs[-1].start()
+        d_own[j][...] = d_own[j][...] + y_chip[j]
 
     for c in sent:
         c.wait_send()
-    wait(outs)
-
-
-def _grad_kernel(xg, q, act, du, dv, y, dg, dw1, dw3, dw2, y_out, dg_out):
+
+
+def _grad_kernel(xg, q, act, du, dv, dg, dw1, dw3, dw2, dg_out):
     for i in range(xg.shape[0]):
         dw1[i] = _dot(xg[i], du[i], DIM0)
         dw3[i] = _dot(xg[i], dv[i], DIM0)
         dw2[i] = _dot(act[i], q[i], DIM0)
-    y_out[...] = y[...]
     dg_out[...] = dg[...]
 
 
@@ -410,23 +397,24 @@
         small = (n_src, top, td)
         whole = pl.BlockSpec(memory_space=pltpu.VMEM)
         flops = 2 * el * er * dm * fh * 6
-        xg, q, act, du, dv, y, dg, dx0, dx1, dx2, dx3 = pl.pallas_call(
+        xg, q, act, du, dv, dg, y_here, dx_here, to_x, to_y, to_xy = pl.pallas_call(
             _core_kernel,
             name='moe_core',
             out_shape=[vmem((el, er, dm), BF), vmem((el, er, dm), BF)] + [vmem((el, er, fh), BF)] * 3
-            + [vmem(block, BF), vmem((top, td), F32)] + [sds(block, F32)] * 4,
+            + [vmem((top, td), F32), vmem(block, F32), vmem(block, F32)]
+            + [vmem((td + td // 2, dm), F32)] * 2 + [vmem(block, F32)],
             in_specs=[ANY] * 7,
-            out_specs=[whole] * 7 + [ANY] * 4,
+            out_specs=[whole] * 11,
             scratch_shapes=[
                 vmem((n_src,) + block, BF), vmem((n_src,) + block, BF), vmem(small, jnp.int32), vmem(small, F32),
                 vmem((el, er, dm), BF),
                 vmem((n_src, el * ROWS, td), BF), vmem((n_src, td, el * ROWS), BF), vmem((n_src, 3 * td, el * ROWS), BF),
                 vmem((SLOTS, dm, fh), BF), vmem((SLOTS, dm, fh), BF), vmem((SLOTS, fh, dm), BF),
-                vmem((4,) + block, F32), vmem((4,) + block, F32), vmem((4,) + block, F32), vmem((6, td // 2, dm), F32),
-                vmem((4,) + block, F32), vmem(small, F32), vmem(small, F32),
-                dma((4,)), dma((3, SLOTS)), dma((4,)),
+                vmem((4,) + block, F32), vmem((4,) + block, F32), vmem((4,) + block, F32), vmem((4, td // 2, dm), F32),
+                vmem(small, F32), vmem(small, F32),
+                dma((4,)), dma((3, SLOTS)),
                 dma((16,)), dma((16,)), dma((8,)), dma((8,)), dma((8,)), dma((8,)), dma((8,)), dma((8,)),
-                dma((4,)), dma((4,)), dma((6,)), dma((6,)), dma((4,)), dma((4,)), dma((8,)), dma((8,)),
+                dma((4,)), dma((4,)), dma((4,)), dma((4,)), dma((4,)), dma((4,)), dma((8,)), dma((8,)),
             ],
             compiler_params=pltpu.CompilerParams(collective_id=0, has_side_effects=True, vmem_limit_bytes=CORE_VMEM << 20),
             cost_estimate=pl.CostEstimate(flops=flops, bytes_accessed=88 << 20, transcendentals=0),
@@ -435,22 +423,23 @@
         def swap(a, k):
             return lax.ppermute(a, ep, [(i, i ^ k) for i in range(n_src)])
 
-        far = [swap(dx3, 6), swap(dx1, 2), swap(dx2, 4)]
+        from_xy, from_x, from_y = swap(to_xy, 6), swap(to_x, 2), swap(to_y, 4)
         per = 2
         spec = lambda a, b: pl.BlockSpec((per, a, b), lambda i: (i, 0, 0))
         once = lambda a, b: pl.BlockSpec((a, b), lambda i: (0, 0))
 
-        dw1, dw3, dw2, y, dg = pl.pallas_call(
+        dw1, dw3, dw2, dg = pl.pallas_call(
             _grad_kernel,
             name='moe_grad',
             grid=(el // per,),
-            out_shape=[sds((el, dm, fh), F32), sds((el, dm, fh), F32), sds((el, fh, dm), F32), sds(block, BF), sds((top, td), F32)],
-            in_specs=[spec(er, dm), spec(er, dm), spec(er, fh), spec(er, fh), spec(er, fh), once(td, dm), once(top, td)],
-            out_specs=[spec(dm, fh), spec(dm, fh), spec(fh, dm), once(td, dm), once(top, td)],
+            out_shape=[sds((el, dm, fh), F32), sds((el, dm, fh), F32), sds((el, fh, dm), F32), sds((top, td), F32)],
+            in_specs=[spec(er, dm), spec(er, dm), spec(er, fh), spec(er, fh), spec(er, fh), once(top, td)],
+            out_specs=[spec(dm, fh), spec(dm, fh), spec(fh, dm), once(top, td)],
             compiler_params=pltpu.CompilerParams(vmem_limit_bytes=GRAD_VMEM << 20),
             cost_estimate=pl.CostEstimate(flops=2 * el * er * dm * fh * 3, bytes_accessed=90 << 20, transcendentals=0),
-        )(xg, q, act, du, dv, y, dg)
-        dx = (dx0 + far[0] + far[1] + far[2]).astype(BF)
+        )(xg, q, act, du, dv, dg)
+        dx = (dx_here + from_x[:td] + from_y[:td] + from_xy).astype(BF)
+        y = (y_here + jnp.concatenate([from_y[td:], from_x[td:]])).astype(BF)
         return y, dx, dg.T, dw1, dw3, dw2
 
     return jax.shard_map(body, mesh=mesh, in_specs=(tspec, tspec, tspec, wspec, wspec, wspec, tspec),

time: 92.4 us -> 91.6 us (level)
  Pallas kernels: 87.4 us -> 85.7 us
    pallas_call x1, Pallas kernels: 59.2 us -> 57.6 us  [body(): pl.pallas_call(_core_kernel, name='moe_core', out_shape=[vmem((el, er, dm...]
  transfers between devices with their start and end apart: 3 -> 3, of which waited for: 0 -> 0; matrix products, arithmetic and copies ran while one was open for 0% -> 1% of each run, Pallas kernels for 31% -> 31%
where the time goes in v3:
time: 91.6 us; the launch traced here: 91.5 us
  Pallas kernels  85.7 us (94%)
  starting transfers between devices  3.51 us (4%)
  other arithmetic  1.54 us (2%)
    pallas_call x1, Pallas kernels, body(): pl.pallas_call(_core_kernel, name='moe_core', out_shape=[vmem((el, er, dm...  57.6 us
    pallas_call x1, Pallas kernels, body(): pl.pallas_call(_grad_kernel, name='moe_grad', grid=(el // per,), out_shap...  28.1 us
    ppermute x3, starting transfers between devices, swap(): return lax.ppermute(a, ep, [(i, i ^ k) for i in range(n_src)])  3.51 us
  transfers between devices with their start and end apart: 3, of which 0 were waited for; matrix products, arithmetic and copies ran while one was open for 1% of the time, Pallas kernels for 31%

profile of v3, /device:TPU:0, one launch (start us, length us, event | category | flops | bytes accessed | tf_op | source)
XLA Modules:
  0.0 91.5 jit_solution(8091029281058184117)
XLA Ops:
  0.6 57.6 %moe_core.1 = (bf16[32,128,896]{2,1,0:T(8,128)(2,1)S(1)}, bf16[32,128,896]{2,1,0:T(8,128)(2,1)S(1)}, bf16[32,128,256]{2,1,0:T(8,128)(2,1)S(1)}, bf16[32,128,256]...) custom-call(bf16[128,896]{1,0:T(8,128)(2,1)} %x_hbm.1, ...), custom_call_target="tpu_custom_call" | custom-call | flops 11274289152 | bytes 92274688 | tf_op jit(solution)/shard_map/moe_core/pallas_call | solution.py:400
  58.2 1.3 %collective-permute-start = (f32[192,896]{1,0:T(8,128)S(1)}, f32[192,896]{1,0:T(8,128)S(1)}, u32[]{:S(2)}, u32[]{:S(2)}) collective-permute-start(f32[192,896]{1,0:T(8,128)S(1)} %get-tuple-element.22), channel_id=1, source_target_pairs={{0,4},{1,5},{2,6},{3,7},{4,0},{5,1},{6,2},{7,3}} | collective-permute-start | bytes 2064392 | tf_op jit(solution)/shard_map/ppermute | solution.py:424
  59.5 0.7 collective-permute-start.1
  60.3 1.5 %collective-permute-start.2 = (f32[128,896]{1,0:T(8,128)S(1)}, f32[128,896]{1,0:T(8,128)S(1)}, u32[]{:S(2)}, u32[]{:S(2)}) collective-permute-start(f32[128,896]{1,0:T(8,128)S(1)} %get-tuple-element.25), channel_id=1, source_target_pairs={{0,6},{1,7},{2,4},{3,5},{4,2},{5,3},{6,0},{7,1}} | collective-permute-start | bytes 1376264 | tf_op jit(solution)/shard_map/ppermute | solution.py:424
  61.7 28.1 %moe_grad.1 = (f32[32,896,256]{2,1,0:T(8,128)}, f32[32,896,256]{2,1,0:T(8,128)}, f32[32,256,896]{2,1,0:T(8,128)}, f32[8,128]{1,0:T(8,128)}) custom-call(bf16[32,128,896]{2,1,0:T(8,128)(2,1)S(1)} %get-tuple-element.26.xg, bf16[32,128,896]{2,1,0:T(8,128)(2,1)S(1)} %get-tuple-element.27.q, bf16[32,128,256]{2,1,0:T(8,128)(2,1)S(1)} %get-tuple-element.28.act, ...), custom_call_target="tpu_custom_call" | custom-call | flops 5637144576 | bytes 94371840 | tf_op jit(solution)/shard_map/moe_grad/pallas_call | solution.py:431
  89.9 0.0 collective-permute-done
  89.9 0.0 collective-permute-done.1
  89.9 0.7 fusion.2
  90.7 0.0 collective-permute-done.2
  90.7 0.8 fusion.1
  (2 shorter events, 0.0 us)
Async XLA Ops:
  58.2 31.6 %collective-permute-start = (f32[192,896]{1,0:T(8,128)S(1)}, f32[192,896]{1,0:T(8,128)S(1)}, u32[]{:S(2)}, u32[]{:S(2)}) collective-permute-start(f32[192,896]{1,0:T(8,128)S(1)} %get-tuple-element.22), channel_id=1, source_target_pairs={{0,4},{1,5},{2,6},{3,7},{4,0},{5,1},{6,2},{7,3}} | collective-permute-start | bytes 2064392 | tf_op jit(solution)/shard_map/ppermute | solution.py:424
  59.5 30.3 %collective-permute-start.1 = (f32[192,896]{1,0:T(8,128)S(1)}, f32[192,896]{1,0:T(8,128)S(1)}, u32[]{:S(2)}, u32[]{:S(2)}) collective-permute-start(f32[192,896]{1,0:T(8,128)S(1)} %get-tuple-element.23), channel_id=1, source_target_pairs={{0,2},{1,3},{2,0},{3,1},{4,6},{5,7},{6,4},{7,5}} | collective-permute-start | bytes 2064392 | tf_op jit(solution)/shard_map/ppermute | solution.py:424
  60.3 30.4 %collective-permute-start.2 = (f32[128,896]{1,0:T(8,128)S(1)}, f32[128,896]{1,0:T(8,128)S(1)}, u32[]{:S(2)}, u32[]{:S(2)}) collective-permute-start(f32[128,896]{1,0:T(8,128)S(1)} %get-tuple-element.25), channel_id=1, source_target_pairs={{0,6},{1,7},{2,4},{3,5},{4,2},{5,3},{6,0},{7,1}} | collective-permute-start | bytes 1376264 | tf_op jit(solution)/shard_map/ppermute | solution.py:424

commit v4 on v3

--- a/solution.py
+++ b/solution.py
@@ -15,6 +15,7 @@
 CORE_VMEM = 41
 GRAD_VMEM = 14
 GROUP = 4
+PARTS = 4
 DIM0 = (((0,), (0,)), ((), ()))
 DIM1 = (((1,), (1,)), ((), ()))
 ANY = pl.BlockSpec(memory_space=pl.ANY)
@@ -149,7 +150,6 @@
         s = peer(k)[1]
         xg[:, rows_of(s), :] = _dot(onehot[s], x_all[s]).astype(BF).reshape(el, ROWS, dm)
 
-    dispatch_x(0)
     near_x, near_y, diagonal = peer(2)[1], peer(4)[1], peer(6)[1]
     x_wait(near_x, 0)
     x_send(near_x, 0, 4)
@@ -157,6 +157,7 @@
     x_wait(near_y, 1)
     x_send(near_y, 1, 2)
     x_send(near_y, 1, 1)
+    dispatch_x(0)
     for h in range(2):
         x_wait(peer(1)[1], h)
     dispatch_x(1)
@@ -231,9 +232,12 @@
     for e in group(groups - 1):
         forward_out(e)
 
-    def y_part(s):
-        z = _dot(gate3_t[s], o[:, rows_of(s), :].reshape(el * ROWS, dm))
-        return z[:td] + z[td:2 * td] + z[2 * td:]
+    def y_part(s, out):
+        def columns(c):
+            n = min(256, dm - c)
+            z = _dot(gate3_t[s], o[:, rows_of(s), pl.ds(c, n)].reshape(el * ROWS, n))
+            out[:, pl.ds(c, n)] = z[:td] + z[td:2 * td] + z[2 * td:]
+        return [functools.partial(columns, c) for c in range(0, dm, 256)]
 
     def y_half(j, h):
         return y_own.at[j, pl.ds(h * half, half)]
@@ -245,30 +249,12 @@
         arrive(y_far.at[i], yf_s.at[i], yf_r.at[i])
         return y_half(j, h)[...] + y_far[i]
 
-    chip = []
-    for j in range(4):
-        y_send[j] = y_part(peer(2 * j + 1)[1])
-        chip.append(send(y_send.at[j], y_chip.at[j], yc_s.at[j], yc_r.at[j], 1))
-    for k in (2, 4, 6):
-        s = peer(k)[1]
-        arrive(dy_all.at[s], ys_sem.at[k], yr_sem.at[s])
-        sent.append(send(dy_all.at[s], dy_all.at[s], ys_sem.at[k + 1], yr_sem.at[s], 1))
-    for j in range(4):
-        y_own[j] = y_part(peer(2 * j)[1])
-    for j in (3, 1, 2, 0):
-        arrive(y_chip.at[j], yc_s.at[j], yc_r.at[j])
-        y_own[j] = y_own[j] + y_chip[j]
-        if j == 2:
-            far_send(3, 0, 0, 2)
-            far_send(3, 1, 1, 4)
-            far_send(1, 0, 2, 2)
-            far_send(2, 1, 3, 4)
-
     def dispatch_dy(s):
         gate = gates_of(s)
         dgt = []
-        part = el // 4
-        for h in range(4):
+        part = el // PARTS
+
+        def rows(h):
             es = slice(h * part, (h + 1) * part)
             hot = onehot[s, h * part * ROWS:(h + 1) * part * ROWS, :]
             d = _dot(hot, dy_all[s])
@@ -279,16 +265,50 @@
             g = jnp.broadcast_to(gate[es][:, None, :], (part, ROWS, td)).reshape(part * ROWS, td)
             g = jnp.sum(hot * g, axis=1, keepdims=True)
             q[es, rows_of(s), :] = (g * d).astype(BF).reshape(part, ROWS, dm)
-        dgt = jnp.concatenate(dgt, axis=0)
-        for j in range(top):
-            m = route_all[s, j:j + 1, :] == experts
-            dg_send[s, j:j + 1, :] = jnp.sum(jnp.where(m, dgt, 0.0), axis=0, keepdims=True)
-
-    for k in (0, 1, 2, 4, 6, 3, 5, 7):
+
+        def finish():
+            total = jnp.concatenate(dgt, axis=0)
+            for j in range(top):
+                m = route_all[s, j:j + 1, :] == experts
+                dg_send[s, j:j + 1, :] = jnp.sum(jnp.where(m, total, 0.0), axis=0, keepdims=True)
+
+        return [functools.partial(rows, h) for h in range(PARTS)] + [finish]
+
+    def together(y_steps, d_steps):
+        each = -(-len(d_steps) // len(y_steps))
+        for i, step in enumerate(y_steps):
+            step()
+            for d_step in d_steps[i * each:(i + 1) * each]:
+                d_step()
+
+    chip = []
+    for i, k in enumerate((0, 1, 2, 4, 6, 3, 5, 7)):
+        j = i % 4
+        if i == 1:
+            arrive(dy_all.at[peer(1)[1]], ys_sem.at[1], yr_sem.at[peer(1)[1]])
+        if i == 2:
+            for n in (2, 4, 6):
+                s = peer(n)[1]
+                arrive(dy_all.at[s], ys_sem.at[n], yr_sem.at[s])
+                sent.append(send(dy_all.at[s], dy_all.at[s], ys_sem.at[n + 1], yr_sem.at[s], 1))
+        if i == 5:
+            for n in (3, 5, 7):
+                s = peer(n)[1]
+                arrive(dy_all.at[s], ys_sem.at[n], yr_sem.at[s])
+        to_chip = i < 4
+        together(y_part(peer(2 * j + 1 if to_chip else 2 * j)[1], (y_send if to_chip else y_own).at[j]), dispatch_dy(peer(k)[1]))
+        if to_chip:
+            chip.append(send(y_send.at[j], y_chip.at[j], yc_s.at[j], yc_r.at[j], 1))
+    for j in (3, 1, 2, 0):
+        arrive(y_chip.at[j], yc_s.at[j], yc_r.at[j])
+        y_own[j] = y_own[j] + y_chip[j]
+        if j == 2:
+            far_send(3, 0, 0, 2)
+            far_send(3, 1, 1, 4)
+            far_send(1, 0, 2, 2)
+            far_send(2, 1, 3, 4)
+    for k in range(n_src):
         s = peer(k)[1]
-        if k in (1, 3, 5, 7):
-            arrive(dy_all.at[s], ys_sem.at[k], yr_sem.at[s])
-        dispatch_dy(s)
         if k:
             sent.append(send(dg_send.at[s], dg_all.at[me], gs_sem.at[k], gr_sem.at[me], k))
         else:
@@ -299,8 +319,12 @@
         uf = u[e].astype(F32)
         vf = v[e].astype(F32)
         sg = jax.nn.sigmoid(uf)
-        u[e] = (da * vf * sg * (1 + uf * (1 - sg))).astype(BF)
-        v[e] = (da * (uf * sg)).astype(BF)
+        return (da * vf * sg * (1 + uf * (1 - sg))).astype(BF), (da * (uf * sg)).astype(BF)
+
+    def backward_hiddens(es):
+        for e, (du, dv) in [(e, backward_hidden(e)) for e in es]:
+            u[e] = du
+            v[e] = dv
 
     def backward_out(e):
         slot = e % SLOTS
@@ -327,14 +351,12 @@
         ready(down, now)
         for e in prev:
             backward_out(e)
-        for e in now:
-            backward_hidden(e)
+        backward_hiddens(now)
         refill(up, prev)
         refill(down, now)
         return 0
 
-    for e in down_group(0):
-        backward_hidden(e)
+    backward_hiddens(down_group(0))
     refill(down, down_group(0))
     lax.fori_loop(1, groups, backward, 0)
     ready(up, down_group(groups - 1))

time: 91.6 us -> 89 us (0.972)
  Pallas kernels: 85.7 us -> 83.1 us
    pallas_call x1, Pallas kernels: 57.6 us -> 55 us  [body(): pl.pallas_call(_core_kernel, name='moe_core', out_shape=[vmem((el, er, dm...]
  transfers between devices with their start and end apart: 3 -> 3, of which waited for: 0 -> 0; matrix products, arithmetic and copies ran while one was open for 1% -> 1% of each run, Pallas kernels for 31% -> 32%
where the time goes in v4:
time: 89 us; the launch traced here: 88.9 us
  Pallas kernels  83.1 us (93%)
  starting transfers between devices  3.51 us (4%)
  other arithmetic  1.54 us (2%)
    pallas_call x1, Pallas kernels, body(): pl.pallas_call(_core_kernel, name='moe_core', out_shape=[vmem((el, er, dm...  55 us
    pallas_call x1, Pallas kernels, body(): pl.pallas_call(_grad_kernel, name='moe_grad', grid=(el // per,), out_shap...  28.1 us
    ppermute x3, starting transfers between devices, swap(): return lax.ppermute(a, ep, [(i, i ^ k) for i in range(n_src)])  3.51 us
  transfers between devices with their start and end apart: 3, of which 0 were waited for; matrix products, arithmetic and copies ran while one was open for 1% of the time, Pallas kernels for 32%

profile of v4, /device:TPU:0, one launch (start us, length us, event | category | flops | bytes accessed | tf_op | source)
XLA Modules:
  0.0 88.9 jit_solution(11888336513082679425)
XLA Ops:
  0.6 55.0 %moe_core.1 = (bf16[32,128,896]{2,1,0:T(8,128)(2,1)S(1)}, bf16[32,128,896]{2,1,0:T(8,128)(2,1)S(1)}, bf16[32,128,256]{2,1,0:T(8,128)(2,1)S(1)}, bf16[32,128,256]...) custom-call(bf16[128,896]{1,0:T(8,128)(2,1)} %x_hbm.1, ...), custom_call_target="tpu_custom_call" | custom-call | flops 11274289152 | bytes 92274688 | tf_op jit(solution)/shard_map/moe_core/pallas_call | solution.py:422
  55.6 1.3 %collective-permute-start = (f32[192,896]{1,0:T(8,128)S(1)}, f32[192,896]{1,0:T(8,128)S(1)}, u32[]{:S(2)}, u32[]{:S(2)}) collective-permute-start(f32[192,896]{1,0:T(8,128)S(1)} %get-tuple-element.22), channel_id=1, source_target_pairs={{0,4},{1,5},{2,6},{3,7},{4,0},{5,1},{6,2},{7,3}} | collective-permute-start | bytes 2064392 | tf_op jit(solution)/shard_map/ppermute | solution.py:446
  57.0 0.7 collective-permute-start.1
  57.7 1.5 %collective-permute-start.2 = (f32[128,896]{1,0:T(8,128)S(1)}, f32[128,896]{1,0:T(8,128)S(1)}, u32[]{:S(2)}, u32[]{:S(2)}) collective-permute-start(f32[128,896]{1,0:T(8,128)S(1)} %get-tuple-element.25), channel_id=1, source_target_pairs={{0,6},{1,7},{2,4},{3,5},{4,2},{5,3},{6,0},{7,1}} | collective-permute-start | bytes 1376264 | tf_op jit(solution)/shard_map/ppermute | solution.py:446
  59.1 28.1 %moe_grad.1 = (f32[32,896,256]{2,1,0:T(8,128)}, f32[32,896,256]{2,1,0:T(8,128)}, f32[32,256,896]{2,1,0:T(8,128)}, f32[8,128]{1,0:T(8,128)}) custom-call(bf16[32,128,896]{2,1,0:T(8,128)(2,1)S(1)} %get-tuple-element.26.xg, bf16[32,128,896]{2,1,0:T(8,128)(2,1)S(1)} %get-tuple-element.27.q, bf16[32,128,256]{2,1,0:T(8,128)(2,1)S(1)} %get-tuple-element.28.act, ...), custom_call_target="tpu_custom_call" | custom-call | flops 5637144576 | bytes 94371840 | tf_op jit(solution)/shard_map/moe_grad/pallas_call | solution.py:453
  87.3 0.0 collective-permute-done
  87.3 0.0 collective-permute-done.1
  87.3 0.7 fusion.2
  88.1 0.0 collective-permute-done.2
  88.1 0.8 fusion.1
  (2 shorter events, 0.0 us)
Async XLA Ops:
  55.6 31.6 %collective-permute-start = (f32[192,896]{1,0:T(8,128)S(1)}, f32[192,896]{1,0:T(8,128)S(1)}, u32[]{:S(2)}, u32[]{:S(2)}) collective-permute-start(f32[192,896]{1,0:T(8,128)S(1)} %get-tuple-element.22), channel_id=1, source_target_pairs={{0,4},{1,5},{2,6},{3,7},{4,0},{5,1},{6,2},{7,3}} | collective-permute-start | bytes 2064392 | tf_op jit(solution)/shard_map/ppermute | solution.py:446
  57.0 30.3 %collective-permute-start.1 = (f32[192,896]{1,0:T(8,128)S(1)}, f32[192,896]{1,0:T(8,128)S(1)}, u32[]{:S(2)}, u32[]{:S(2)}) collective-permute-start(f32[192,896]{1,0:T(8,128)S(1)} %get-tuple-element.23), channel_id=1, source_target_pairs={{0,2},{1,3},{2,0},{3,1},{4,6},{5,7},{6,4},{7,5}} | collective-permute-start | bytes 2064392 | tf_op jit(solution)/shard_map/ppermute | solution.py:446
  57.7 30.4 %collective-permute-start.2 = (f32[128,896]{1,0:T(8,128)S(1)}, f32[128,896]{1,0:T(8,128)S(1)}, u32[]{:S(2)}, u32[]{:S(2)}) collective-permute-start(f32[128,896]{1,0:T(8,128)S(1)} %get-tuple-element.25), channel_id=1, source_target_pairs={{0,6},{1,7},{2,4},{3,5},{4,2},{5,3},{6,0},{7,1}} | collective-permute-start | bytes 1376264 | tf_op jit(solution)/shard_map/ppermute | solution.py:446

commit v5 on v4

--- a/solution.py
+++ b/solution.py
@@ -14,6 +14,7 @@
 SLOTS = 12
 CORE_VMEM = 41
 GRAD_VMEM = 14
+FINISH_VMEM = 6
 GROUP = 4
 PARTS = 4
 DIM0 = (((0,), (0,)), ((), ()))
@@ -29,11 +30,12 @@
                  xg, q, act, u, v, dg_out, y_here, dx_here, to_x, to_y, to_xy,
                  x_all, dy_all, route_all, gate_all, o, onehot, onehot_t, gate3_t,
                  w1, w3, w2, y_send, y_own, y_chip, y_far, dg_send, dg_all,
-                 in_sem, w_sem,
+                 in_sem, w_sem, e_sem,
                  xs_sem, xr_sem, ys_sem, yr_sem, ts_sem, tr_sem, gts_sem, gtr_sem,
                  yc_s, yc_r, yf_s, yf_r, dc_s, dc_r, gs_sem, gr_sem):
     row, col, core = lax.axis_index('row'), lax.axis_index('col'), lax.axis_index('core')
     el, dm, fh = w1_hbm.shape
+    late = el - el // w2_hbm.shape[1]
     td = x_hbm.shape[0]
     top = route_hbm.shape[0]
     n_src = x_all.shape[0]
@@ -66,11 +68,17 @@
     def down(e):
         return [pltpu.make_async_copy(w2_hbm.at[e], w2.at[e % SLOTS], w_sem.at[2, e % SLOTS])]
 
+    def down_early(e):
+        n = w2_hbm.shape[1]
+        return [pltpu.make_async_copy(w2_hbm.at[e], q.at[pl.ds((e - late) * n, n)], e_sem.at[e - late])]
+
     barrier = pltpu.get_barrier_semaphore()
     for k in range(1, n_src):
         pl.semaphore_signal(barrier, inc=1, device_id=peer(k)[0], device_id_type=MESH)
     for e in range(SLOTS):
         start(up(e) + down(e))
+    for e in range(late, el):
+        start(down_early(e))
     pl.semaphore_wait(barrier, n_src - 1)
 
     def send(src, dst, s_sem, r_sem, k):
@@ -197,27 +205,30 @@
         uf = ue.astype(F32)
         act[e] = (uf * jax.nn.sigmoid(uf) * ve.astype(F32)).astype(BF)
 
-    def forward_out(e):
-        o[e] = _dot(act[e], w2[e % SLOTS]).astype(BF)
-
-    def ahead(copies, es):
+    def forward_out(e, early):
+        n = w2_hbm.shape[1]
+        w = q[pl.ds((e - late) * n, n)] if early else w2[e % SLOTS]
+        o[e] = _dot(act[e], w.reshape(fh, dm)).astype(BF)
+
+    def ahead(copies, es, end):
         for e in es:
-            @pl.when(e + SLOTS < el)
+            @pl.when(e + SLOTS < end)
             def _():
                 start(copies(e + SLOTS))
 
-    def forward(p, _):
+    def forward(early, p, _):
         prev, now = group(p - 1), group(p)
         for e in prev:
-            wait(down(e))
+            wait(down_early(e) if early else down(e))
         for e in now:
             wait(up(e))
         for e in prev:
-            forward_out(e)
+            forward_out(e, early)
         for e in now:
             forward_hidden(e)
-        ahead(down, prev)
-        ahead(up, now)
+        if not early:
+            ahead(down, prev, late)
+        ahead(up, now, el)
         return 0
 
     for e in group(0):
@@ -226,11 +237,14 @@
         forward_hidden(e)
     for e in group(0):
         start(up(e + SLOTS))
-    lax.fori_loop(1, groups, forward, 0)
+    lax.fori_loop(1, late // GROUP + 1, functools.partial(forward, False), 0)
+    lax.fori_loop(late // GROUP + 1, groups, functools.partial(forward, True), 0)
+    for e in range(el - SLOTS, el):
+        start(down(e))
     for e in group(groups - 1):
-        wait(down(e))
+        wait(down_early(e))
     for e in group(groups - 1):
-        forward_out(e)
+        forward_out(e, True)
 
     def y_part(s, out):
         def columns(c):
@@ -315,7 +329,7 @@
             dg_all[me] = dg_send[s]
 
     def backward_hidden(e):
-        da = _dot(q[e], w2[e % SLOTS], DIM1).astype(BF).astype(F32)
+        da = _dot(q[e], w2[e % SLOTS].reshape(fh, dm), DIM1).astype(BF).astype(F32)
         uf = u[e].astype(F32)
         vf = v[e].astype(F32)
         sg = jax.nn.sigmoid(uf)
@@ -348,7 +362,8 @@
     def backward(p, _):
         prev, now = down_group(p - 1), down_group(p)
         ready(up, prev)
-        ready(down, now)
+        for e in now:
+            wait(down(e))
         for e in prev:
             backward_out(e)
         backward_hiddens(now)
@@ -356,6 +371,8 @@
         refill(down, now)
         return 0
 
+    for e in down_group(0):
+        wait(down(e))
     backward_hiddens(down_group(0))
     refill(down, down_group(0))
     lax.fori_loop(1, groups, backward, 0)
@@ -399,6 +416,14 @@
         dw3[i] = _dot(xg[i], dv[i], DIM0)
         dw2[i] = _dot(act[i], q[i], DIM0)
     dg_out[...] = dg[...]
+
+
+def _finish_kernel(y_here, dx_here, from_x, from_y, from_xy, y, dx):
+    td = y.shape[0]
+    half = td // 2
+    dx[...] = (dx_here[...] + from_x[:td, :] + from_y[:td, :] + from_xy[...]).astype(BF)
+    y[:half, :] = (y_here[:half, :] + from_y[td:, :]).astype(BF)
+    y[half:, :] = (y_here[half:, :] + from_x[td:, :]).astype(BF)
 
 
 def solution(mesh):
@@ -431,16 +456,16 @@
                 vmem((n_src,) + block, BF), vmem((n_src,) + block, BF), vmem(small, jnp.int32), vmem(small, F32),
                 vmem((el, er, dm), BF),
                 vmem((n_src, el * ROWS, td), BF), vmem((n_src, td, el * ROWS), BF), vmem((n_src, 3 * td, el * ROWS), BF),
-                vmem((SLOTS, dm, fh), BF), vmem((SLOTS, dm, fh), BF), vmem((SLOTS, fh, dm), BF),
+                vmem((SLOTS, dm, fh), BF), vmem((SLOTS, dm, fh), BF), vmem((SLOTS, fh // er, er, dm), BF),
                 vmem((4,) + block, F32), vmem((4,) + block, F32), vmem((4,) + block, F32), vmem((4, td // 2, dm), F32),
                 vmem(small, F32), vmem(small, F32),
-                dma((4,)), dma((3, SLOTS)),
+                dma((4,)), dma((3, SLOTS)), dma((el,)),
                 dma((16,)), dma((16,)), dma((8,)), dma((8,)), dma((8,)), dma((8,)), dma((8,)), dma((8,)),
                 dma((4,)), dma((4,)), dma((4,)), dma((4,)), dma((4,)), dma((4,)), dma((8,)), dma((8,)),
             ],
             compiler_params=pltpu.CompilerParams(collective_id=0, has_side_effects=True, vmem_limit_bytes=CORE_VMEM << 20),
             cost_estimate=pl.CostEstimate(flops=flops, bytes_accessed=88 << 20, transcendentals=0),
-        )(x, dy, route_idx.T, gates.T, w1, w3, w2)
+        )(x, dy, route_idx.T, gates.T, w1, w3, w2.reshape(el, fh // er, er, dm))
 
         def swap(a, k):
             return lax.ppermute(a, ep, [(i, i ^ k) for i in range(n_src)])
@@ -460,8 +485,14 @@
             compiler_params=pltpu.CompilerParams(vmem_limit_bytes=GRAD_VMEM << 20),
             cost_estimate=pl.CostEstimate(flops=2 * el * er * dm * fh * 3, bytes_accessed=90 << 20, transcendentals=0),
         )(xg, q, act, du, dv, dg)
-        dx = (dx_here + from_x[:td] + from_y[:td] + from_xy).astype(BF)
-        y = (y_here + jnp.concatenate([from_y[td:], from_x[td:]])).astype(BF)
+        y, dx = pl.pallas_call(
+            _finish_kernel,
+            name='moe_finish',
+            out_shape=[sds(block, BF), sds(block, BF)],
+            in_specs=[whole] * 5,
+            out_specs=[whole] * 2,
+            compiler_params=pltpu.CompilerParams(vmem_limit_bytes=FINISH_VMEM << 20),
+        )(y_here, dx_here, from_x, from_y, from_xy)
         return y, dx, dg.T, dw1, dw3, dw2
 
     return jax.shard_map(body, mesh=mesh, in_specs=(tspec, tspec, tspec, wspec, wspec, wspec, tspec),

time: 89 us -> 87.2 us (0.980)
  other arithmetic: 1.54 us -> 0 us
    convert_element_type x2 -> x0, other arithmetic: 1.54 us -> none  [the longest x1 0.81 us: body(): dx = (dx_here + from_x[:td] + from_y[:td] + from_xy).astype(BF)]
    pallas_call x1, Pallas kernels: 55 us -> 53.9 us  [body(): pl.pallas_call(_core_kernel, name='moe_core', out_shape=[vmem((el, er, dm...]
  transfers between devices with their start and end apart: 3 -> 3, of which waited for: 0 -> 0; matrix products, arithmetic and copies ran while one was open for 1% -> 0% of each run, Pallas kernels for 32% -> 32%
where the time goes in v5:
time: 87.2 us; the launch traced here: 87 us
  Pallas kernels  82.9 us (95%)
  starting transfers between devices  3.51 us (4%)
    pallas_call x1, Pallas kernels, body(): pl.pallas_call(_core_kernel, name='moe_core', out_shape=[vmem((el, er, dm...  53.9 us
    pallas_call x1, Pallas kernels, body(): pl.pallas_call(_grad_kernel, name='moe_grad', grid=(el // per,), out_shap...  28.1 us
    ppermute x3, starting transfers between devices, swap(): return lax.ppermute(a, ep, [(i, i ^ k) for i in range(n_src)])  3.51 us
  transfers between devices with their start and end apart: 3, of which 0 were waited for; matrix products, arithmetic and copies ran while one was open for 0% of the time, Pallas kernels for 32%

profile of v5, /device:TPU:0, one launch (start us, length us, event | category | flops | bytes accessed | tf_op | source)
XLA Modules:
  0.0 87.0 jit_solution(3397441745780242401)
XLA Ops:
  0.6 53.9 %moe_core.1 = (bf16[32,128,896]{2,1,0:T(8,128)(2,1)S(1)}, bf16[32,128,896]{2,1,0:T(8,128)(2,1)S(1)}, bf16[32,128,256]{2,1,0:T(8,128)(2,1)S(1)}, bf16[32,128,256]...) custom-call(bf16[128,896]{1,0:T(8,128)(2,1)} %x_hbm.1, ...), custom_call_target="tpu_custom_call" | custom-call | flops 11274289152 | bytes 92274688 | tf_op jit(solution)/shard_map/moe_core/pallas_call | solution.py:447
  54.5 1.5 %collective-permute-start = (f32[192,896]{1,0:T(8,128)S(1)}, f32[192,896]{1,0:T(8,128)S(1)}, u32[]{:S(2)}, u32[]{:S(2)}) collective-permute-start(f32[192,896]{1,0:T(8,128)S(1)} %get-tuple-element.25), channel_id=1, source_target_pairs={{0,2},{1,3},{2,0},{3,1},{4,6},{5,7},{6,4},{7,5}} | collective-permute-start | bytes 2064392 | tf_op jit(solution)/shard_map/ppermute | solution.py:471
  56.0 0.6 collective-permute-start.1
  56.5 1.5 %collective-permute-start.2 = (f32[128,896]{1,0:T(8,128)S(1)}, f32[128,896]{1,0:T(8,128)S(1)}, u32[]{:S(2)}, u32[]{:S(2)}) collective-permute-start(f32[128,896]{1,0:T(8,128)S(1)} %get-tuple-element.27), channel_id=1, source_target_pairs={{0,6},{1,7},{2,4},{3,5},{4,2},{5,3},{6,0},{7,1}} | collective-permute-start | bytes 1376264 | tf_op jit(solution)/shard_map/ppermute | solution.py:471
  58.0 28.1 %moe_grad.1 = (f32[32,896,256]{2,1,0:T(8,128)}, f32[32,896,256]{2,1,0:T(8,128)}, f32[32,256,896]{2,1,0:T(8,128)}, f32[8,128]{1,0:T(8,128)}) custom-call(bf16[32,128,896]{2,1,0:T(8,128)(2,1)S(1)} %get-tuple-element.30.xg, bf16[32,128,896]{2,1,0:T(8,128)(2,1)S(1)} %get-tuple-element.31.q, bf16[32,128,256]{2,1,0:T(8,128)(2,1)S(1)} %get-tuple-element.32.act, ...), custom_call_target="tpu_custom_call" | custom-call | flops 5637144576 | bytes 94371840 | tf_op jit(solution)/shard_map/moe_grad/pallas_call | solution.py:478
  86.1 0.0 collective-permute-done.2.from_xy
  86.1 0.0 collective-permute-done.from_x
  86.1 0.0 collective-permute-done.1.from_y
  86.2 0.9 %moe_finish.1 = (bf16[128,896]{1,0:T(8,128)(2,1)}, bf16[128,896]{1,0:T(8,128)(2,1)}) custom-call(f32[128,896]{1,0:T(8,128)S(1)} %get-tuple-element.23.y_here, f32[128,896]{1,0:T(8,128)S(1)} %get-tuple-element.24.dx_here, f32[192,896]{1,0:T(8,128)S(1)} %collective-permute-done.from_x, f32[192,896]{1,0:T(8,128)S(1)} %collective-permute-done.1.from_y, ...), custom_call_target="tpu_custom_call" | custom-call | tf_op jit(solution)/shard_map/moe_finish/pallas_call | solution.py:488
Async XLA Ops:
  54.5 31.6 %collective-permute-start = (f32[192,896]{1,0:T(8,128)S(1)}, f32[192,896]{1,0:T(8,128)S(1)}, u32[]{:S(2)}, u32[]{:S(2)}) collective-permute-start(f32[192,896]{1,0:T(8,128)S(1)} %get-tuple-element.25), channel_id=1, source_target_pairs={{0,2},{1,3},{2,0},{3,1},{4,6},{5,7},{6,4},{7,5}} | collective-permute-start | bytes 2064392 | tf_op jit(solution)/shard_map/ppermute | solution.py:471
  56.0 30.2 %collective-permute-start.1 = (f32[192,896]{1,0:T(8,128)S(1)}, f32[192,896]{1,0:T(8,128)S(1)}, u32[]{:S(2)}, u32[]{:S(2)}) collective-permute-start(f32[192,896]{1,0:T(8,128)S(1)} %get-tuple-element.26), channel_id=1, source_target_pairs={{0,4},{1,5},{2,6},{3,7},{4,0},{5,1},{6,2},{7,3}} | collective-permute-start | bytes 2064392 | tf_op jit(solution)/shard_map/ppermute | solution.py:471
  56.5 29.6 %collective-permute-start.2 = (f32[128,896]{1,0:T(8,128)S(1)}, f32[128,896]{1,0:T(8,128)S(1)}, u32[]{:S(2)}, u32[]{:S(2)}) collective-permute-start(f32[128,896]{1,0:T(8,128)S(1)} %get-tuple-element.27), channel_id=1, source_target_pairs={{0,6},{1,7},{2,4},{3,5},{4,2},{5,3},{6,0},{7,1}} | collective-permute-start | bytes 1376264 | tf_op jit(solution)/shard_map/ppermute | solution.py:471

commit v6 on v5

--- a/solution.py
+++ b/solution.py
@@ -296,21 +296,21 @@
                 d_step()
 
     chip = []
-    for i, k in enumerate((0, 1, 2, 4, 6, 3, 5, 7)):
+    for i, ks in enumerate(((0,), (1,), (), (2,), (4,), (6,), (3, 5), (7,))):
         j = i % 4
-        if i == 1:
+        if 1 in ks:
             arrive(dy_all.at[peer(1)[1]], ys_sem.at[1], yr_sem.at[peer(1)[1]])
-        if i == 2:
+        if 2 in ks:
             for n in (2, 4, 6):
                 s = peer(n)[1]
                 arrive(dy_all.at[s], ys_sem.at[n], yr_sem.at[s])
                 sent.append(send(dy_all.at[s], dy_all.at[s], ys_sem.at[n + 1], yr_sem.at[s], 1))
-        if i == 5:
+        if 3 in ks:
             for n in (3, 5, 7):
                 s = peer(n)[1]
                 arrive(dy_all.at[s], ys_sem.at[n], yr_sem.at[s])
         to_chip = i < 4
-        together(y_part(peer(2 * j + 1 if to_chip else 2 * j)[1], (y_send if to_chip else y_own).at[j]), dispatch_dy(peer(k)[1]))
+        together(y_part(peer(2 * j + 1 if to_chip else 2 * j)[1], (y_send if to_chip else y_own).at[j]), [step for k in ks for step in dispatch_dy(peer(k)[1])])
         if to_chip:
             chip.append(send(y_send.at[j], y_chip.at[j], yc_s.at[j], yc_r.at[j], 1))
     for j in (3, 1, 2, 0):

time: 87.2 us -> 87 us (level)
  no operation moved by 1% of the time
where the time goes in v6:
time: 87 us; the launch traced here: 86.9 us
  Pallas kernels  82.8 us (95%)
  starting transfers between devices  3.51 us (4%)
    pallas_call x1, Pallas kernels, body(): pl.pallas_call(_core_kernel, name='moe_core', out_shape=[vmem((el, er, dm...  53.7 us
    pallas_call x1, Pallas kernels, body(): pl.pallas_call(_grad_kernel, name='moe_grad', grid=(el // per,), out_shap...  28.1 us
    ppermute x3, starting transfers between devices, swap(): return lax.ppermute(a, ep, [(i, i ^ k) for i in range(n_src)])  3.51 us
  transfers between devices with their start and end apart: 3, of which 0 were waited for; matrix products, arithmetic and copies ran while one was open for 0% of the time, Pallas kernels for 32%

profile of v6, /device:TPU:0, one launch (start us, length us, event | category | flops | bytes accessed | tf_op | source)
XLA Modules:
  0.0 86.9 jit_solution(9242522458997399289)
XLA Ops:
  0.6 53.7 %moe_core.1 = (bf16[32,128,896]{2,1,0:T(8,128)(2,1)S(1)}, bf16[32,128,896]{2,1,0:T(8,128)(2,1)S(1)}, bf16[32,128,256]{2,1,0:T(8,128)(2,1)S(1)}, bf16[32,128,256]...) custom-call(bf16[128,896]{1,0:T(8,128)(2,1)} %x_hbm.1, ...), custom_call_target="tpu_custom_call" | custom-call | flops 11274289152 | bytes 92274688 | tf_op jit(solution)/shard_map/moe_core/pallas_call | solution.py:447
  54.4 1.4 %collective-permute-start = (f32[192,896]{1,0:T(8,128)S(1)}, f32[192,896]{1,0:T(8,128)S(1)}, u32[]{:S(2)}, u32[]{:S(2)}) collective-permute-start(f32[192,896]{1,0:T(8,128)S(1)} %get-tuple-element.25), channel_id=1, source_target_pairs={{0,2},{1,3},{2,0},{3,1},{4,6},{5,7},{6,4},{7,5}} | collective-permute-start | bytes 2064392 | tf_op jit(solution)/shard_map/ppermute | solution.py:471
  55.8 0.6 collective-permute-start.1
  56.5 1.4 %collective-permute-start.2 = (f32[128,896]{1,0:T(8,128)S(1)}, f32[128,896]{1,0:T(8,128)S(1)}, u32[]{:S(2)}, u32[]{:S(2)}) collective-permute-start(f32[128,896]{1,0:T(8,128)S(1)} %get-tuple-element.27), channel_id=1, source_target_pairs={{0,6},{1,7},{2,4},{3,5},{4,2},{5,3},{6,0},{7,1}} | collective-permute-start | bytes 1376264 | tf_op jit(solution)/shard_map/ppermute | solution.py:471
  57.9 28.1 %moe_grad.1 = (f32[32,896,256]{2,1,0:T(8,128)}, f32[32,896,256]{2,1,0:T(8,128)}, f32[32,256,896]{2,1,0:T(8,128)}, f32[8,128]{1,0:T(8,128)}) custom-call(bf16[32,128,896]{2,1,0:T(8,128)(2,1)S(1)} %get-tuple-element.30.xg, bf16[32,128,896]{2,1,0:T(8,128)(2,1)S(1)} %get-tuple-element.31.q, bf16[32,128,256]{2,1,0:T(8,128)(2,1)S(1)} %get-tuple-element.32.act, ...), custom_call_target="tpu_custom_call" | custom-call | flops 5637144576 | bytes 94371840 | tf_op jit(solution)/shard_map/moe_grad/pallas_call | solution.py:478
  86.0 0.0 collective-permute-done.2.from_xy
  86.0 0.0 collective-permute-done.from_x
  86.0 0.0 collective-permute-done.1.from_y
  86.0 0.9 %moe_finish.1 = (bf16[128,896]{1,0:T(8,128)(2,1)}, bf16[128,896]{1,0:T(8,128)(2,1)}) custom-call(f32[128,896]{1,0:T(8,128)S(1)} %get-tuple-element.23.y_here, f32[128,896]{1,0:T(8,128)S(1)} %get-tuple-element.24.dx_here, f32[192,896]{1,0:T(8,128)S(1)} %collective-permute-done.from_x, f32[192,896]{1,0:T(8,128)S(1)} %collective-permute-done.1.from_y, ...), custom_call_target="tpu_custom_call" | custom-call | tf_op jit(solution)/shard_map/moe_finish/pallas_call | solution.py:488
Async XLA Ops:
  54.4 31.6 %collective-permute-start = (f32[192,896]{1,0:T(8,128)S(1)}, f32[192,896]{1,0:T(8,128)S(1)}, u32[]{:S(2)}, u32[]{:S(2)}) collective-permute-start(f32[192,896]{1,0:T(8,128)S(1)} %get-tuple-element.25), channel_id=1, source_target_pairs={{0,2},{1,3},{2,0},{3,1},{4,6},{5,7},{6,4},{7,5}} | collective-permute-start | bytes 2064392 | tf_op jit(solution)/shard_map/ppermute | solution.py:471
  55.8 30.2 %collective-permute-start.1 = (f32[192,896]{1,0:T(8,128)S(1)}, f32[192,896]{1,0:T(8,128)S(1)}, u32[]{:S(2)}, u32[]{:S(2)}) collective-permute-start(f32[192,896]{1,0:T(8,128)S(1)} %get-tuple-element.26), channel_id=1, source_target_pairs={{0,4},{1,5},{2,6},{3,7},{4,0},{5,1},{6,2},{7,3}} | collective-permute-start | bytes 2064392 | tf_op jit(solution)/shard_map/ppermute | solution.py:471
  56.5 29.6 %collective-permute-start.2 = (f32[128,896]{1,0:T(8,128)S(1)}, f32[128,896]{1,0:T(8,128)S(1)}, u32[]{:S(2)}, u32[]{:S(2)}) collective-permute-start(f32[128,896]{1,0:T(8,128)S(1)} %get-tuple-element.27), channel_id=1, source_target_pairs={{0,6},{1,7},{2,4},{3,5},{4,2},{5,3},{6,0},{7,1}} | collective-permute-start | bytes 1376264 | tf_op jit(solution)/shard_map/ppermute | solution.py:471

commit v7 on v6

--- a/solution.py
+++ b/solution.py
@@ -175,15 +175,17 @@
     x_send(near_y, 0, 1)
     for k in (2, 4):
         dispatch_x(k)
-    for k in (3, 5):
-        for h in range(2):
-            x_wait(peer(k)[1], h)
-        dispatch_x(k)
+    for h in range(2):
+        x_wait(peer(3)[1], h)
+    dispatch_x(3)
     for h in range(2):
         x_wait(diagonal, h)
         x_send(diagonal, h, 1)
     for k in (2, 4, 6, 1):
         sent.append(send(dy_all.at[me], dy_all.at[me], ys_sem.at[k], yr_sem.at[me], k))
+    for h in range(2):
+        x_wait(peer(5)[1], h)
+    dispatch_x(5)
     dispatch_x(6)
     for h in range(2):
         x_wait(peer(7)[1], h)

time: 87 us -> 87 us (level)
  no operation moved by 1% of the time
where the time goes in v7:
time: 87 us; the launch traced here: 86.9 us
  Pallas kernels  82.8 us (95%)
  starting transfers between devices  3.51 us (4%)
    pallas_call x1, Pallas kernels, body(): pl.pallas_call(_core_kernel, name='moe_core', out_shape=[vmem((el, er, dm...  53.7 us
    pallas_call x1, Pallas kernels, body(): pl.pallas_call(_grad_kernel, name='moe_grad', grid=(el // per,), out_shap...  28.1 us
    ppermute x3, starting transfers between devices, swap(): return lax.ppermute(a, ep, [(i, i ^ k) for i in range(n_src)])  3.51 us
  transfers between devices with their start and end apart: 3, of which 0 were waited for; matrix products, arithmetic and copies ran while one was open for 0% of the time, Pallas kernels for 32%

profile of v7, /device:TPU:0, one launch (start us, length us, event | category | flops | bytes accessed | tf_op | source)
XLA Modules:
  0.0 86.9 jit_solution(1325339458979242630)
XLA Ops:
  0.6 53.7 %moe_core.1 = (bf16[32,128,896]{2,1,0:T(8,128)(2,1)S(1)}, bf16[32,128,896]{2,1,0:T(8,128)(2,1)S(1)}, bf16[32,128,256]{2,1,0:T(8,128)(2,1)S(1)}, bf16[32,128,256]...) custom-call(bf16[128,896]{1,0:T(8,128)(2,1)} %x_hbm.1, ...), custom_call_target="tpu_custom_call" | custom-call | flops 11274289152 | bytes 92274688 | tf_op jit(solution)/shard_map/moe_core/pallas_call | solution.py:449
  54.4 1.4 %collective-permute-start = (f32[192,896]{1,0:T(8,128)S(1)}, f32[192,896]{1,0:T(8,128)S(1)}, u32[]{:S(2)}, u32[]{:S(2)}) collective-permute-start(f32[192,896]{1,0:T(8,128)S(1)} %get-tuple-element.25), channel_id=1, source_target_pairs={{0,2},{1,3},{2,0},{3,1},{4,6},{5,7},{6,4},{7,5}} | collective-permute-start | bytes 2064392 | tf_op jit(solution)/shard_map/ppermute | solution.py:473
  55.8 0.6 collective-permute-start.1
  56.4 1.5 %collective-permute-start.2 = (f32[128,896]{1,0:T(8,128)S(1)}, f32[128,896]{1,0:T(8,128)S(1)}, u32[]{:S(2)}, u32[]{:S(2)}) collective-permute-start(f32[128,896]{1,0:T(8,128)S(1)} %get-tuple-element.27), channel_id=1, source_target_pairs={{0,6},{1,7},{2,4},{3,5},{4,2},{5,3},{6,0},{7,1}} | collective-permute-start | bytes 1376264 | tf_op jit(solution)/shard_map/ppermute | solution.py:473
  57.9 28.1 %moe_grad.1 = (f32[32,896,256]{2,1,0:T(8,128)}, f32[32,896,256]{2,1,0:T(8,128)}, f32[32,256,896]{2,1,0:T(8,128)}, f32[8,128]{1,0:T(8,128)}) custom-call(bf16[32,128,896]{2,1,0:T(8,128)(2,1)S(1)} %get-tuple-element.30.xg, bf16[32,128,896]{2,1,0:T(8,128)(2,1)S(1)} %get-tuple-element.31.q, bf16[32,128,256]{2,1,0:T(8,128)(2,1)S(1)} %get-tuple-element.32.act, ...), custom_call_target="tpu_custom_call" | custom-call | flops 5637144576 | bytes 94371840 | tf_op jit(solution)/shard_map/moe_grad/pallas_call | solution.py:480
  86.0 0.0 collective-permute-done.2.from_xy
  86.0 0.0 collective-permute-done.from_x
  86.0 0.0 collective-permute-done.1.from_y
  86.0 0.9 %moe_finish.1 = (bf16[128,896]{1,0:T(8,128)(2,1)}, bf16[128,896]{1,0:T(8,128)(2,1)}) custom-call(f32[128,896]{1,0:T(8,128)S(1)} %get-tuple-element.23.y_here, f32[128,896]{1,0:T(8,128)S(1)} %get-tuple-element.24.dx_here, f32[192,896]{1,0:T(8,128)S(1)} %collective-permute-done.from_x, f32[192,896]{1,0:T(8,128)S(1)} %collective-permute-done.1.from_y, ...), custom_call_target="tpu_custom_call" | custom-call | tf_op jit(solution)/shard_map/moe_finish/pallas_call | solution.py:490
Async XLA Ops:
  54.4 31.6 %collective-permute-start = (f32[192,896]{1,0:T(8,128)S(1)}, f32[192,896]{1,0:T(8,128)S(1)}, u32[]{:S(2)}, u32[]{:S(2)}) collective-permute-start(f32[192,896]{1,0:T(8,128)S(1)} %get-tuple-element.25), channel_id=1, source_target_pairs={{0,2},{1,3},{2,0},{3,1},{4,6},{5,7},{6,4},{7,5}} | collective-permute-start | bytes 2064392 | tf_op jit(solution)/shard_map/ppermute | solution.py:473
  55.8 30.2 %collective-permute-start.1 = (f32[192,896]{1,0:T(8,128)S(1)}, f32[192,896]{1,0:T(8,128)S(1)}, u32[]{:S(2)}, u32[]{:S(2)}) collective-permute-start(f32[192,896]{1,0:T(8,128)S(1)} %get-tuple-element.26), channel_id=1, source_target_pairs={{0,4},{1,5},{2,6},{3,7},{4,0},{5,1},{6,2},{7,3}} | collective-permute-start | bytes 2064392 | tf_op jit(solution)/shard_map/ppermute | solution.py:473
  56.4 29.6 %collective-permute-start.2 = (f32[128,896]{1,0:T(8,128)S(1)}, f32[128,896]{1,0:T(8,128)S(1)}, u32[]{:S(2)}, u32[]{:S(2)}) collective-permute-start(f32[128,896]{1,0:T(8,128)S(1)} %get-tuple-element.27), channel_id=1, source_target_pairs={{0,6},{1,7},{2,4},{3,5},{4,2},{5,3},{6,0},{7,1}} | collective-permute-start | bytes 1376264 | tf_op jit(solution)/shard_map/ppermute | solution.py:473
